TPU v7x, 256 devices: a whole 4x4x8 slice. The times are simulated.
256 devices in a mesh: tm: 64 (over x, z, core), env: 4 (over y).
Axes of the slice: x: 4, y: 4, z: 8, core: 2. Of those that a mesh axis runs over, the one named last changes fastest.
Arguments:
- init_state: float32 [70, 1024], P(None, 'env'), may hold values from -6 to 6
- torque: float32 [256, 35, 1024], P('tm', None, 'env'), may hold values from -192 to 192
- contact: int32 [256, 1024], P('tm', 'env'), may hold values 0 or 1
- mass_inverse: float32 [128, 35, 35], P('tm'), may hold values from -0.014 to 1.5, as said below
- stiffness: float32 [35], replicated, may hold values from 10 to 100
- damping: float32 [35], replicated, may hold values from 0.5 to 5
- gravity: float32 [35], replicated, may hold values from 1 to 10
- contact_stiffness: float32 [35], replicated, may hold values from 20 to 100
- contact_damping: float32 [35], replicated, may hold values from 0.5 to 3
Outputs:
- final_states: float32 [128, 70, 1024], P('tm', None, 'env')
- corrections: float32 [3, 1024], P(None, 'env')
Inputs may be any that keep to these rules, and one draw needn't show every extreme that they name: `mass_inverse`: each matrix is symmetric, and each diagonal entry exceeds the sum of the magnitudes of the other entries of its row.
All inputs are finite; a program needn't handle non-finite values. No bound on the sum of `contact` on one device may be relied on, other than what follows from the above.
Results may differ from a plain program's by a relative error of at most 0.00025.
Values sent between devices are 32-bit elements; how exact they have to be, the bound alone decides.
No kernel may reach another device: no remote copies, remote signals or barrier semaphores. Data moves between devices by JAX's collectives and lax.ppermute only.
A program may use at most 64 MiB of HBM per device.

v0:
```python
import jax
import jax.numpy as jnp
from jax import lax
from jax.sharding import Mesh
from jax.sharding import PartitionSpec as P

DOF = 35
HS = 2
SUB = 32
ITERS = 3
TM = ("tm_0", "tm_1", "tm_2")


step_length = 0.05


def sent_to_all(value, axis):
    copies = jnp.broadcast_to(value, (lax.axis_size(axis), *value.shape))
    return lax.all_to_all(copies, axis, split_axis=0, concat_axis=0, tiled=True)


def of_everyone(value, axis):
    return sent_to_all(value, axis).sum(axis=0)


def neutral_like(value, identity):
    return jax.tree.map(
        lambda part, zero: jnp.zeros_like(part) + jnp.asarray(zero, part.dtype), value, identity
    )


def prefix_by_axis(value, axes, combine, identity):
    before = start = neutral_like(value, identity)
    running = value
    for axis in reversed(axes):
        count, index = (lax.axis_size(axis), lax.axis_index(axis))
        pieces = jax.tree.map(lambda part: lax.all_gather(part, axis), running)
        inside, running = (start, start)
        for k in range(count):
            passed = k < index
            running = combine(running, jax.tree.map(lambda part: part[k], pieces))
            inside = jax.tree.map(lambda new, old: jnp.where(passed, new, old), running, inside)
        before = combine(inside, before)
    return before


def taken_together(value, axis):
    return sent_to_all(value, axis).max(axis=0)


def exact_dot(left, right):
    return jnp.dot(left, right, precision=lax.Precision.HIGHEST, preferred_element_type=jnp.float32)


def coarse_one(state_now, torque_steps, mean_steps, inverse, params):
    stiffness, damping, gravity, contact_stiffness, contact_damping = params
    joint_pos = state_now[:DOF]
    joint_vel = state_now[DOF:]
    for step_pos in range(HS):
        spring = (stiffness + gravity + mean_steps[step_pos] * contact_stiffness)[:, None]
        friction = (damping + mean_steps[step_pos] * contact_damping)[:, None]
        force = torque_steps[step_pos] - spring * joint_pos - friction * joint_vel
        joint_vel = joint_vel + step_length * exact_dot(inverse, force)
        joint_pos = joint_pos + step_length * joint_vel
    return jnp.concatenate([joint_pos, joint_vel], axis=0)


def fine_one(state_now, torque_steps, contact_steps, inverse, params):
    stiffness, damping, gravity, contact_stiffness, contact_damping = params
    fine_dt = step_length / SUB
    joint_pair = (state_now[:DOF], state_now[DOF:])
    for step_pos in range(HS):
        torque_here = torque_steps[step_pos]
        contact_here = contact_steps[step_pos][None, :]

        def substep(counter, pair_now):
            joint_pos, joint_vel = pair_now
            force = (
                torque_here
                - stiffness[:, None] * joint_pos
                - damping[:, None] * joint_vel
                - gravity[:, None] * jnp.sin(joint_pos)
                - contact_here
                * (contact_stiffness[:, None] * joint_pos + contact_damping[:, None] * joint_vel)
            )
            joint_vel = joint_vel + fine_dt * exact_dot(inverse, force)
            joint_pos = joint_pos + fine_dt * joint_vel
            return (joint_pos, joint_vel)

        joint_pair = lax.fori_loop(0, SUB, substep, joint_pair, unroll=min(8, SUB))
    return jnp.concatenate([joint_pair[0], joint_pair[1]], axis=0)


def compose(former, latter):
    return (exact_dot(latter[0], former[0]), exact_dot(latter[0], former[1]) + latter[1])


def shards(
    init_state,
    torque,
    contact,
    mass_inverse,
    stiffness,
    damping,
    gravity,
    contact_stiffness,
    contact_damping,
):
    params = (stiffness, damping, gravity, contact_stiffness, contact_damping)
    local_slices = mass_inverse.shape[0]
    env_local = init_state.shape[1]
    state_rows = init_state.shape[0]
    torque_steps = torque.reshape(local_slices, HS, DOF, env_local)
    contact_float = contact.astype(jnp.float32)
    contact_steps = contact_float.reshape(local_slices, HS, env_local)
    totals = of_everyone(jnp.sum(contact_float, axis=1), "env")
    mean_steps = (totals / (env_local * lax.axis_size("env"))).reshape(local_slices, HS)
    eye_state = jnp.eye(state_rows, dtype=jnp.float32)
    zero_shift = jnp.zeros((state_rows, env_local), jnp.float32)
    no_force = jnp.zeros((local_slices, HS, DOF, 1), jnp.float32)
    step_maps = jax.vmap(coarse_one, in_axes=(None, 0, 0, 0, None))(
        eye_state, no_force, mean_steps, mass_inverse, params
    )
    coarse_free = jax.vmap(coarse_one, in_axes=(0, 0, 0, 0, None))(
        jnp.zeros((local_slices, state_rows, env_local), jnp.float32),
        torque_steps,
        mean_steps,
        mass_inverse,
        params,
    )
    device_map = eye_state
    for slot_pos in range(local_slices):
        device_map = exact_dot(step_maps[slot_pos], device_map)

    def sweep(offsets):
        local_shift = zero_shift
        for slot_pos in range(local_slices):
            local_shift = exact_dot(step_maps[slot_pos], local_shift) + offsets[slot_pos]
        prefix_map, prefix_shift = prefix_by_axis(
            (device_map, local_shift), TM, compose, (eye_state, zero_shift)
        )
        entry = exact_dot(prefix_map, init_state) + prefix_shift
        start_list = []
        end_list = []
        current = entry
        for slot_pos in range(local_slices):
            start_list.append(current)
            current = exact_dot(step_maps[slot_pos], current) + offsets[slot_pos]
            end_list.append(current)
        return (jnp.stack(start_list), jnp.stack(end_list))

    starts, ends = sweep(coarse_free)
    fine_all = jax.vmap(fine_one, in_axes=(0, 0, 0, 0, None))
    records = []
    for iteration in range(ITERS):
        fine_end = fine_all(starts, torque_steps, contact_steps, mass_inverse, params)
        jumps = fine_end - jnp.einsum(
            "sij,sje->sie", step_maps, starts, precision=lax.Precision.HIGHEST
        )
        new_starts, new_ends = sweep(jumps)
        local_max = jnp.max(jnp.sqrt(jnp.sum((new_ends - ends) ** 2, axis=1)), axis=0)
        records.append(local_max)
        starts, ends = (new_starts, new_ends)
    corrections = jnp.stack(records)
    corrections = taken_together(corrections, TM)
    return (ends, corrections)


def solution(mesh):
    torus = Mesh(mesh.devices.reshape(4, 8, 2, mesh.shape["env"]), ("tm_0", "tm_1", "tm_2", "env"))
    return jax.shard_map(
        shards,
        mesh=torus,
        in_specs=(
            P(None, "env"),
            P(TM, None, "env"),
            P(TM, "env"),
            P(TM, None, None),
            P(),
            P(),
            P(),
            P(),
            P(),
        ),
        out_specs=(P(TM, None, "env"), P(None, "env")),
        check_vma=False,
    )
```

profile of v0, /device:TPU:1, one launch (start us, length us, event | category | flops | bytes accessed | tf_op | source)
XLA Modules:
  0.0 363.3 jit_solution(5527427069862304610)
XLA Ops:
  0.6 0.8 convert_reduce_fusion
  1.5 0.6 broadcast_in_dim.6
  2.1 5.0 %all-to-all-start = ((f32[4,1,4]{2,1,0:T(1,128)}), f32[4,1,4]{2,1,0:T(1,128)S(1)}, u32[]{:S(2)}, u32[]{:S(2)}) async-start(f32[4,1,4]{2,1,0:T(1,128)} %broadcast_in_dim.6), calls=%async_computation | async-start | bytes 4096 | tf_op jit(solution)/shard_map/all_to_all | solution.py:19
  7.1 0.7 copy-done.8
  7.9 0.7 copy-done.6
  8.9 0.6 copy-done.4
  9.6 1.5 all-to-all-done
  11.5 0.6 copy-done.1
  13.2 4.1 %all-gather.15 = f32[2,70,70]{2,1,0:T(8,128)S(1)} all-gather(f32[1,70,70]{2,1,0:T(8,128)S(1)} %convolution_bitcast_fusion), channel_id=2, replica_groups=mesh['tm_0'=4,'tm_1'=8,'tm_2'=2,'env'=4] {'tm_2'}, dimensions={0}, use_global_device_ids=true | all-gather | bytes 58800 | tf_op jit(solution)/shard_map/all_gather | solution.py:37
  18.0 22.1 %all-gather.16 = f32[8,70,70]{2,1,0:T(8,128)S(1)} all-gather(f32[1,70,70]{2,1,0:T(8,128)S(1)} %bitcast.1051), channel_id=3, replica_groups=mesh['tm_0'=4,'tm_1'=8,'tm_2'=2,'env'=4] {'tm_1'}, dimensions={0}, use_global_device_ids=true | all-gather | bytes 176400 | tf_op jit(solution)/shard_map/all_gather | solution.py:37
  42.0 9.5 %all-gather.17 = f32[4,70,70]{2,1,0:T(8,128)S(1)} all-gather(f32[1,70,70]{2,1,0:T(8,128)S(1)} %bitcast.1050), channel_id=4, replica_groups=mesh['tm_0'=4,'tm_1'=8,'tm_2'=2,'env'=4] {'tm_0'}, dimensions={0}, use_global_device_ids=true | all-gather | bytes 98000 | tf_op jit(solution)/shard_map/all_gather | solution.py:37
  53.0 10.7 %all-gather.18 = f32[2,70,256]{2,1,0:T(8,128)S(1)} all-gather(f32[1,70,256]{2,1,0:T(8,128)S(1)} %fusion.1029), channel_id=5, replica_groups=mesh['tm_0'=4,'tm_1'=8,'tm_2'=2,'env'=4] {'tm_2'}, dimensions={0}, use_global_device_ids=true | all-gather | bytes 215040 | tf_op jit(solution)/shard_map/all_gather | solution.py:37
  64.3 19.9 %all-gather.19 = f32[8,70,256]{2,1,0:T(8,128)S(1)} all-gather(f32[1,70,256]{2,1,0:T(8,128)S(1)} %bitcast.1047), channel_id=6, replica_groups=mesh['tm_0'=4,'tm_1'=8,'tm_2'=2,'env'=4] {'tm_1'}, dimensions={0}, use_global_device_ids=true | all-gather | bytes 645120 | tf_op jit(solution)/shard_map/all_gather | solution.py:37
  86.4 9.6 %all-gather.20 = f32[4,70,256]{2,1,0:T(8,128)S(1)} all-gather(f32[1,70,256]{2,1,0:T(8,128)S(1)} %bitcast.1041), channel_id=7, replica_groups=mesh['tm_0'=4,'tm_1'=8,'tm_2'=2,'env'=4] {'tm_0'}, dimensions={0}, use_global_device_ids=true | all-gather | bytes 358400 | tf_op jit(solution)/shard_map/all_gather | solution.py:37
  98.1 17.2 %while.72 = (s32[]{:T(128)}, f32[2,35,256]{2,1,0:T(8,128)S(1)}, f32[2,35,256]{2,1,0:T(8,128)S(1)}, f32[35]{0:T(128)S(1)}, f32[2,35,256]{2,1,0:T(8,128)S(1)}, /*i...) while((s32[]{:T(128)}, f32[2,35,256]{2,1,0:T(8,128)S(1)}, ...), condition=%wide.region_3.4_spmd, body=%wide.region_2.3_spmd.sunk | while | flops 62504960 | bytes 2680981 | solution.py:90
  98.7 0.5 multiply_add_fusion.107
  99.7 0.5 multiply_add_fusion.108
  101.9 0.5 multiply_add_fusion.110
  102.9 0.5 multiply_add_fusion.107
  104.0 0.5 multiply_add_fusion.108
  106.2 0.5 multiply_add_fusion.110
  107.2 0.5 multiply_add_fusion.107
  108.3 0.5 multiply_add_fusion.108
  111.5 0.5 multiply_add_fusion.107
  114.7 0.5 multiply_add_fusion.110
  115.3 17.2 %while.73 = (s32[]{:T(128)}, f32[2,35,256]{2,1,0:T(8,128)S(1)}, f32[2,35,256]{2,1,0:T(8,128)S(1)}, f32[35]{0:T(128)S(1)}, f32[2,35,256]{2,1,0:T(8,128)S(1)}, /*i...) while((s32[]{:T(128)}, f32[2,35,256]{2,1,0:T(8,128)S(1)}, ...), condition=%wide.region_5.6_spmd, body=%wide.region_4.5_spmd.sunk | while | flops 62504960 | bytes 2680981 | solution.py:90
  133.0 10.3 %all-gather.21 = f32[2,70,256]{2,1,0:T(8,128)S(1)} all-gather(f32[1,70,256]{2,1,0:T(8,128)S(1)} %fusion.1025), channel_id=8, replica_groups=mesh['tm_0'=4,'tm_1'=8,'tm_2'=2,'env'=4] {'tm_2'}, dimensions={0}, use_global_device_ids=true | all-gather | bytes 215040 | tf_op jit(solution)/shard_map/all_gather | solution.py:37
  143.5 19.6 %all-gather.22 = f32[8,70,256]{2,1,0:T(8,128)S(1)} all-gather(f32[1,70,256]{2,1,0:T(8,128)S(1)} %bitcast.1048), channel_id=9, replica_groups=mesh['tm_0'=4,'tm_1'=8,'tm_2'=2,'env'=4] {'tm_1'}, dimensions={0}, use_global_device_ids=true | all-gather | bytes 645120 | tf_op jit(solution)/shard_map/all_gather | solution.py:37
  164.8 9.6 %all-gather.23 = f32[4,70,256]{2,1,0:T(8,128)S(1)} all-gather(f32[1,70,256]{2,1,0:T(8,128)S(1)} %bitcast.1044), channel_id=10, replica_groups=mesh['tm_0'=4,'tm_1'=8,'tm_2'=2,'env'=4] {'tm_0'}, dimensions={0}, use_global_device_ids=true | all-gather | bytes 358400 | tf_op jit(solution)/shard_map/all_gather | solution.py:37
  175.9 17.2 %while.74 = (s32[]{:T(128)}, f32[2,35,256]{2,1,0:T(8,128)S(1)}, f32[2,35,256]{2,1,0:T(8,128)S(1)}, f32[35]{0:T(128)S(1)}, f32[2,35,256]{2,1,0:T(8,128)S(1)}, /*i...) while((s32[]{:T(128)}, f32[2,35,256]{2,1,0:T(8,128)S(1)}, ...), condition=%wide.region_7.8_spmd, body=%wide.region_6.7_spmd.sunk | while | flops 62504960 | bytes 2680981 | solution.py:90
  177.6 0.5 multiply_add_fusion.116
  180.8 0.5 multiply_add_fusion.115
  181.8 0.5 multiply_add_fusion.116
  185.1 0.5 multiply_add_fusion.115
  186.1 0.5 multiply_add_fusion.116
  189.4 0.5 multiply_add_fusion.115
  190.4 0.5 multiply_add_fusion.116
  192.6 0.5 multiply_add_fusion.118
  193.1 17.2 %while.75 = (s32[]{:T(128)}, f32[2,35,256]{2,1,0:T(8,128)S(1)}, f32[2,35,256]{2,1,0:T(8,128)S(1)}, f32[35]{0:T(128)S(1)}, f32[2,35,256]{2,1,0:T(8,128)S(1)}, /*i...) while((s32[]{:T(128)}, f32[2,35,256]{2,1,0:T(8,128)S(1)}, ...), condition=%wide.region_9.10_spmd, body=%wide.region_8.9_spmd.sunk | while | flops 62504960 | bytes 2680981 | solution.py:90
  210.8 11.0 %all-gather.24 = f32[2,70,256]{2,1,0:T(8,128)S(1)} all-gather(f32[1,70,256]{2,1,0:T(8,128)S(1)} %fusion.1021), channel_id=11, replica_groups=mesh['tm_0'=4,'tm_1'=8,'tm_2'=2,'env'=4] {'tm_2'}, dimensions={0}, use_global_device_ids=true | all-gather | bytes 215040 | tf_op jit(solution)/shard_map/all_gather | solution.py:37
  222.0 19.5 %all-gather.25 = f32[8,70,256]{2,1,0:T(8,128)S(1)} all-gather(f32[1,70,256]{2,1,0:T(8,128)S(1)} %bitcast.1049), channel_id=12, replica_groups=mesh['tm_0'=4,'tm_1'=8,'tm_2'=2,'env'=4] {'tm_1'}, dimensions={0}, use_global_device_ids=true | all-gather | bytes 645120 | tf_op jit(solution)/shard_map/all_gather | solution.py:37
  243.2 9.7 %all-gather.26 = f32[4,70,256]{2,1,0:T(8,128)S(1)} all-gather(f32[1,70,256]{2,1,0:T(8,128)S(1)} %bitcast.1045), channel_id=13, replica_groups=mesh['tm_0'=4,'tm_1'=8,'tm_2'=2,'env'=4] {'tm_0'}, dimensions={0}, use_global_device_ids=true | all-gather | bytes 358400 | tf_op jit(solution)/shard_map/all_gather | solution.py:37
  254.4 17.2 %while.76 = (s32[]{:T(128)}, f32[2,35,256]{2,1,0:T(8,128)S(1)}, f32[2,35,256]{2,1,0:T(8,128)S(1)}, f32[35]{0:T(128)S(1)}, f32[2,35,256]{2,1,0:T(8,128)S(1)}, /*i...) while((s32[]{:T(128)}, f32[2,35,256]{2,1,0:T(8,128)S(1)}, ...), condition=%wide.region_11.12_spmd, body=%wide.region_10.11_spmd.sunk | while | flops 62504960 | bytes 2680981 | solution.py:90
  255.0 0.5 multiply_add_fusion.123
  256.0 0.5 multiply_add_fusion.124
  258.2 0.5 multiply_add_fusion.126
  259.3 0.5 multiply_add_fusion.123
  260.3 0.5 multiply_add_fusion.124
  263.5 0.5 multiply_add_fusion.123
  264.6 0.5 multiply_add_fusion.124
  266.8 0.5 multiply_add_fusion.126
  267.8 0.5 multiply_add_fusion.123
  268.9 0.5 multiply_add_fusion.124
  271.0 0.5 multiply_add_fusion.126
  271.6 17.1 %while.77 = (s32[]{:T(128)}, f32[2,35,256]{2,1,0:T(8,128)S(1)}, f32[2,35,256]{2,1,0:T(8,128)S(1)}, f32[35]{0:T(128)S(1)}, f32[2,35,256]{2,1,0:T(8,128)S(1)}, /*i...) while((s32[]{:T(128)}, f32[2,35,256]{2,1,0:T(8,128)S(1)}, ...), condition=%wide.region_13.14_spmd, body=%wide.region_12.13_spmd.sunk | while | flops 62504960 | bytes 2680981 | solution.py:90
  279.6 0.5 multiply_add_fusion.130
  289.3 10.9 %all-gather.27 = f32[2,70,256]{2,1,0:T(8,128)S(1)} all-gather(f32[1,70,256]{2,1,0:T(8,128)S(1)} %fusion.1017), channel_id=14, replica_groups=mesh['tm_0'=4,'tm_1'=8,'tm_2'=2,'env'=4] {'tm_2'}, dimensions={0}, use_global_device_ids=true | all-gather | bytes 215040 | tf_op jit(solution)/shard_map/all_gather | solution.py:37
  300.4 19.4 %all-gather.28 = f32[8,70,256]{2,1,0:T(8,128)S(1)} all-gather(f32[1,70,256]{2,1,0:T(8,128)S(1)} %bitcast.1046), channel_id=15, replica_groups=mesh['tm_0'=4,'tm_1'=8,'tm_2'=2,'env'=4] {'tm_1'}, dimensions={0}, use_global_device_ids=true | all-gather | bytes 645120 | tf_op jit(solution)/shard_map/all_gather | solution.py:37
  321.5 9.7 %all-gather.29 = f32[4,70,256]{2,1,0:T(8,128)S(1)} all-gather(f32[1,70,256]{2,1,0:T(8,128)S(1)} %bitcast.1042), channel_id=16, replica_groups=mesh['tm_0'=4,'tm_1'=8,'tm_2'=2,'env'=4] {'tm_0'}, dimensions={0}, use_global_device_ids=true | all-gather | bytes 358400 | tf_op jit(solution)/shard_map/all_gather | solution.py:37
  332.8 0.7 broadcast_in_dim.8
  333.6 16.7 %all-to-all-start.1 = ((f32[64,3,256]{2,1,0:T(4,128)}), f32[64,3,256]{2,1,0:T(4,128)S(1)}, u32[]{:S(2)}, u32[]{:S(2)}) async-start(f32[64,3,256]{2,1,0:T(4,128)} %broadcast_in_dim.8), calls=%async_computation.1 | async-start | bytes 524288 | tf_op jit(solution)/shard_map/all_to_all | solution.py:19
  350.2 0.7 copy.119
  351.0 11.2 %all-to-all-done.1 = f32[64,3,256]{2,1,0:T(4,128)S(1)} async-done(((f32[64,3,256]{2,1,0:T(4,128)}), f32[64,3,256]{2,1,0:T(4,128)S(1)}, u32[]{:S(2)}, u32[]{:S(2)}) %all-to-all-start.1) | async-done | bytes 196640 | tf_op jit(solution)/shard_map/all_to_all | solution.py:19
  362.2 0.7 reduce_max.39
  (305 shorter events, 107.0 us)
Async XLA Ops:
  0.6 96.6 %copy-start = (f32[70,256]{1,0:T(8,128)S(1)}, f32[70,256]{1,0:T(8,128)}, u32[]{:S(2)}) copy-start(f32[70,256]{1,0:T(8,128)} %param.21) | copy-start | bytes 215044
  2.1 9.1 %all-to-all-start = ((f32[4,1,4]{2,1,0:T(1,128)}), f32[4,1,4]{2,1,0:T(1,128)S(1)}, u32[]{:S(2)}, u32[]{:S(2)}) async-start(f32[4,1,4]{2,1,0:T(1,128)} %broadcast_in_dim.6), calls=%async_computation | async-start | bytes 4096 | tf_op jit(solution)/shard_map/all_to_all | solution.py:19
  7.1 0.7 copy-start.8
  7.1 1.5 copy-start.7
  7.8 0.8 copy-start.6
  8.9 0.7 copy-start.4
  8.9 0.7 copy-start.5
  11.4 0.7 copy-start.1
  11.4 0.7 copy-start.2
  11.4 0.7 copy-start.3
  333.6 28.6 %all-to-all-start.1 = ((f32[64,3,256]{2,1,0:T(4,128)}), f32[64,3,256]{2,1,0:T(4,128)S(1)}, u32[]{:S(2)}, u32[]{:S(2)}) async-start(f32[64,3,256]{2,1,0:T(4,128)} %broadcast_in_dim.8), calls=%async_computation.1 | async-start | bytes 524288 | tf_op jit(solution)/shard_map/all_to_all | solution.py:19
where the time goes:
time: 368 us; the launch traced here: 363 us
  blocking collectives  196 us (53%)
  matrix products  122 us (33%)
  starting transfers between devices  21.7 us (6%)
  waiting for transfers between devices  12.8 us (3%)
  local copies, waits for them, and re-layouts  5.6 us (2%)
    all_gather x15, blocking collectives, prefix_by_axis(): pieces = jax.tree.map(lambda part: lax.all_gather(part, axis), running)  196 us
    dot_general x288, matrix products, exact_dot(): jnp.dot(left, right, precision=lax.Precision.HIGHEST, preferred_element_t...  121 us
    all_to_all x2, starting transfers between devices, sent_to_all(): return lax.all_to_all(copies, axis, split_axis=0, concat_axis=0, tiled=True)  21.7 us
    all_to_all x2, waiting for transfers between devices, sent_to_all(): return lax.all_to_all(copies, axis, split_axis=0, concat_axis=0, tiled=True)  12.8 us
  transfers between devices with their start and end apart: 2, of which 2 were waited for; matrix products, arithmetic and copies ran while one was open for 0% of the time, Pallas kernels for 0%

commit v1 on v0

v1 whole, which is shorter than its diff:
```python
import functools
import math

import jax
import jax.numpy as jnp
from jax import lax
from jax.experimental import pallas as pl
from jax.experimental.pallas import tpu as pltpu
from jax.sharding import Mesh
from jax.sharding import PartitionSpec as P

DOF = 35
PAD = 40
HS = 2
SUB = 32
ITERS = 3
GROUP = 4
BLOCKS = 4
CHIPS = 32
STEPS = GROUP * HS
LANES = 128
ENV = 1024
TM = ("x", "z", "c")
PEERS = ("y", "x", "z")

DT = 0.05
FINE = DT / SUB
TURN = 1.0 / (2.0 * math.pi)
SINE = (6.283182595389212, -16.20867027746649, 16.7609745050196, -9.530799181282873, 3.0583252710952205)

ROW_CONTACT = STEPS * PAD
ROW_COUNT = ROW_CONTACT + 8
ROW_INIT = ROW_COUNT + 8
ROW_MASS = 512
CHUNKS = 16
OUT_CHUNKS = 4
VMEM_LIMIT = 56 * 1024 * 1024

f32 = jnp.float32


def lane_index(rows):
    return lax.broadcasted_iota(jnp.int32, (rows, LANES), 1)


def block_transpose(parts):
    lane = lane_index(parts[0].shape[0])
    low = lane < 64
    even = ((lane >> 5) & 1) == 0
    a, b, c, d = parts
    a, c = jnp.where(low, a, pltpu.roll(c, 64, 1)), jnp.where(low, pltpu.roll(a, 64, 1), c)
    b, d = jnp.where(low, b, pltpu.roll(d, 64, 1)), jnp.where(low, pltpu.roll(b, 64, 1), d)
    a, b = jnp.where(even, a, pltpu.roll(b, 32, 1)), jnp.where(even, pltpu.roll(a, 96, 1), b)
    c, d = jnp.where(even, c, pltpu.roll(d, 32, 1)), jnp.where(even, pltpu.roll(c, 96, 1), d)
    return a, b, c, d


def block_spread(value):
    block = lane_index(value.shape[0]) >> 5
    turned = [value] + [pltpu.roll(value, 32 * m, 1) for m in (1, 2, 3)]
    return [
        jnp.where(
            block < 2,
            jnp.where(block == 0, turned[(0 - c) % 4], turned[(1 - c) % 4]),
            jnp.where(block == 2, turned[(2 - c) % 4], turned[(3 - c) % 4]),
        )
        for c in range(4)
    ]


def shifted(value, by):
    group = lane_index(value.shape[0]) & 31
    return jnp.where(group >= by, pltpu.roll(value, by, 1), 0.0)


def pack_kernel(torque, contact, counts, init, mass, out, rows):
    rows[...] = jnp.zeros_like(rows)
    for t in range(STEPS):
        rows[t * PAD : t * PAD + DOF, :] = torque[t]
    rows[ROW_CONTACT : ROW_CONTACT + 8, :] = contact[...]
    rows[ROW_COUNT : ROW_COUNT + 8, :] = jnp.broadcast_to(counts[...], (8, LANES))
    rows[ROW_INIT : ROW_INIT + DOF, :] = init[:DOF, :]
    rows[ROW_INIT + PAD : ROW_INIT + PAD + DOF, :] = init[DOF:, :]
    for c in range(4):
        out[:, c, :] = rows[c * LANES : (c + 1) * LANES, :].T
    for c in range(4, CHUNKS):
        out[:, c, :] = jnp.broadcast_to(mass[c - 4 : c - 3, :], (LANES, LANES))


def state_row(k):
    return k if k < DOF else k + PAD - DOF


def main_kernel(
    recv, par, out, rows, mb, ma, wide, cols, tau_b, stiff_b, damp_b, spring, fric, start, end, shift, diff, pos, vel, force, vec, corr
):
    for c in range(CHUNKS - 1):
        rows[c * LANES : (c + 1) * LANES, :] = recv[:, c, :].T

    def param(i):
        return jnp.broadcast_to(par[:, i : i + 1], (PAD, LANES))

    stiffness, damping, gravity, contact_stiffness, contact_damping = (param(i) for i in range(5))

    mb[...] = jnp.zeros_like(mb)
    ma[...] = jnp.zeros_like(ma)

    def place_mass(k, carry):
        part = rows[pl.ds(pl.multiple_of(ROW_MASS + k * PAD, 8), PAD), :]
        mb[k] = part
        for b, spread in enumerate(block_spread(part)):
            ma[b, k] = spread
        return carry

    lax.fori_loop(0, DOF, place_mass, 0)

    count = rows[ROW_COUNT : ROW_COUNT + 8, :]
    total = count + pltpu.roll(count, 32, 1) + pltpu.roll(count, 64, 1) + pltpu.roll(count, 96, 1)
    mean = total / ENV
    for t in range(STEPS):
        here = mean[t : t + 1, :]
        spring[t] = (stiffness + gravity + here * contact_stiffness) * (FINE * DT)
        fric[t] = (damping + here * contact_damping) * DT

    for j in range(HS):
        turned = block_transpose([rows[(2 * b + j) * PAD : (2 * b + j + 1) * PAD, :] for b in range(GROUP)])
        touch = block_transpose(
            [rows[ROW_CONTACT + 2 * b + j : ROW_CONTACT + 2 * b + j + 1, :] for b in range(GROUP)]
        )
        for e in range(BLOCKS):
            tau_b[j, e] = turned[e] * (FINE * FINE * TURN)
            stiff_b[j, e] = (stiffness + touch[e] * contact_stiffness) * (FINE * FINE)
            damp_b[j, e] = (damping + touch[e] * contact_damping) * FINE

    grav = gravity * (FINE * FINE * TURN)

    def half_step(b, t, q, w, driven):
        pull = spring[t] * q + fric[t] * w
        if driven:
            at = t * PAD if isinstance(t, int) else pl.multiple_of(t * PAD, 8)
            pull = rows[pl.ds(at, PAD), :] * (FINE * DT * TURN) - pull
        else:
            pull = -pull
        vec[0:PAD, :] = pull
        for k in range(DOF):
            w = w + ma[b, k] * vec[k : k + 1, :]
        return q + float(SUB) * w, w

    def slice_step(b, q, w, driven):
        q, w = half_step(b, 2 * b, q, w, driven)
        return half_step(b, 2 * b + 1, q, w, driven)

    def apply_wide(level, value):
        vec[...] = value
        total = None
        for k in range(2 * DOF):
            term = wide[level, k] * vec[state_row(k) : state_row(k) + 1, :]
            total = term if total is None else total + term
        return total

    row80 = lax.broadcasted_iota(jnp.int32, (2 * PAD, LANES), 0)
    col_block = lane_index(2 * PAD) >> 5

    def spread_columns(level, cg, value):
        for c, spread in enumerate(block_spread(value)):
            wide[level, 4 * cg + c] = spread

    def first_columns(cg, carry):
        col = 4 * cg + col_block
        col = jnp.where(col < DOF, col, col + (PAD - DOF))
        unit = jnp.where(row80 == col, 1.0, 0.0)

        def one(b, qw):
            return slice_step(b, qw[0], qw[1], False)

        q, w = lax.fori_loop(0, GROUP, one, (unit[:PAD], unit[PAD:]))
        value = jnp.concatenate([q, w], axis=0)
        cols[cg] = value
        spread_columns(0, cg, value)
        return carry

    lax.fori_loop(0, 18, first_columns, 0)
    for level, by in ((1, 1), (2, 2)):

        def more_columns(cg, carry, level=level, by=by):
            value = apply_wide(level - 1, shifted(cols[cg], by))
            cols[cg] = value
            spread_columns(level, cg, value)
            return carry

        lax.fori_loop(0, 18, more_columns, 0)

    def scan_groups(value):
        value = value + apply_wide(0, shifted(value, 1))
        value = value + apply_wide(1, shifted(value, 2))
        diff[0] = value

        def more(i, running):
            return diff[0] + apply_wide(2, shifted(running, 4))

        return lax.fori_loop(0, 7, more, value)

    first = (lane_index(2 * PAD) & 31) == 0
    init = jnp.where(first, rows[ROW_INIT : ROW_INIT + 2 * PAD, :], 0.0)
    init = jnp.concatenate([init[:PAD] * TURN, init[PAD:] * (FINE * TURN)], axis=0)

    def driven_slice(b, qw):
        return slice_step(b, qw[0], qw[1], True)

    q, w = lax.fori_loop(0, GROUP, driven_slice, (init[:PAD], init[PAD:]))
    ends = scan_groups(jnp.concatenate([q, w], axis=0))
    entry = jnp.where(first, init, shifted(ends, 1))

    def driven_keep(b, qw):
        start[b] = jnp.concatenate(qw, axis=0)
        qw = slice_step(b, qw[0], qw[1], True)
        end[b] = jnp.concatenate(qw, axis=0)
        return qw

    lax.fori_loop(0, GROUP, driven_keep, (entry[:PAD], entry[PAD:]))

    corr[...] = jnp.zeros_like(corr)

    def iteration(it, carry):
        for half, ref in ((0, pos), (PAD, vel)):
            for e, part in enumerate(block_transpose([start[b, half : half + PAD, :] for b in range(GROUP)])):
                ref[e] = part

        def substep(n, carry):
            j = n // SUB
            for e in range(BLOCKS):
                p = pos[e]
                f = p - jnp.round(p)
                s = f * f
                poly = SINE[4] * s + SINE[3]
                for coef in (SINE[2], SINE[1], SINE[0]):
                    poly = poly * s + coef
                sine = (f * (1.0 - 4.0 * s)) * poly
                force[e] = tau_b[j, e] - stiff_b[j, e] * p - damp_b[j, e] * vel[e] - grav * sine
            acc = [vel[e] for e in range(BLOCKS)]
            for k in range(DOF):
                mass = mb[k]
                for e in range(BLOCKS):
                    acc[e] = acc[e] + mass * force[e, k : k + 1, :]
            for e in range(BLOCKS):
                vel[e] = acc[e]
                pos[e] = pos[e] + acc[e]
            return carry

        lax.fori_loop(0, HS * SUB, substep, 0)
        for half, ref in ((0, pos), (PAD, vel)):
            for b, part in enumerate(block_transpose([ref[e] for e in range(BLOCKS)])):
                shift[b, half : half + PAD, :] = part - end[b, half : half + PAD, :]

        def chain(b, qw):
            q, w = slice_step(b, qw[0], qw[1], False)
            return q + shift[b, :PAD, :], w + shift[b, PAD:, :]

        q, w = lax.fori_loop(1, GROUP, chain, (shift[0, :PAD, :], shift[0, PAD:, :]))
        entry = shifted(scan_groups(jnp.concatenate([q, w], axis=0)), 1)

        def keep(b, state):
            q, w, largest = state
            start[b] = start[b] + jnp.concatenate([q, w], axis=0)
            q, w = chain(b, (q, w))
            end[b] = end[b] + jnp.concatenate([q, w], axis=0)
            dq = q * (1.0 / TURN)
            dv = w * (1.0 / (TURN * FINE))
            square = jnp.sum(dq * dq + dv * dv, axis=0, keepdims=True)
            return q, w, jnp.maximum(largest, square)

        _, _, largest = lax.fori_loop(
            0, GROUP, keep, (entry[:PAD], entry[PAD:], jnp.zeros((1, LANES), f32))
        )
        group = lane_index(1) & 31
        for by in (16, 8, 4, 2, 1):
            other = jnp.where(group >= by, pltpu.roll(largest, by, 1), pltpu.roll(largest, LANES - 32 + by, 1))
            largest = jnp.maximum(largest, other)
        corr[pl.ds(it, 1), :] = jnp.sqrt(largest)
        return carry

    lax.fori_loop(0, ITERS, iteration, 0)

    rows[0 : OUT_CHUNKS * LANES, :] = jnp.zeros((OUT_CHUNKS * LANES, LANES), f32)
    for b in range(GROUP):
        rows[b * 2 * PAD : b * 2 * PAD + PAD, :] = end[b, :PAD, :] * (1.0 / TURN)
        rows[b * 2 * PAD + PAD : (b + 1) * 2 * PAD, :] = end[b, PAD:, :] * (1.0 / (TURN * FINE))
    rows[GROUP * 2 * PAD : GROUP * 2 * PAD + 8, :] = corr[...]
    for c in range(OUT_CHUNKS):
        out[:, c, :] = rows[c * LANES : (c + 1) * LANES, :].T


def unpack_kernel(core, recv, mine, other, corr, rows):
    for c in range(OUT_CHUNKS):
        rows[c * LANES : (c + 1) * LANES, :] = recv[:, c, :].T
    here = core[0] * 2
    for ref, base in ((mine, here), (other, 2 - here)):
        for s in range(2):
            at = pl.multiple_of((base + s) * 2 * PAD, 8)
            whole = rows[pl.ds(at, 2 * PAD), :]
            ref[s, 0:DOF, :] = whole[:DOF]
            ref[s, DOF : 2 * DOF, :] = whole[PAD : PAD + DOF]
    corr[...] = rows[GROUP * 2 * PAD : GROUP * 2 * PAD + 8, :]


def params(**more):
    return pltpu.CompilerParams(vmem_limit_bytes=VMEM_LIMIT, **more)


def pack_call(torque, contact, counts, init, mass):
    return pl.pallas_call(
        pack_kernel,
        out_shape=jax.ShapeDtypeStruct((LANES, CHUNKS, LANES), f32),
        scratch_shapes=[pltpu.VMEM((4 * LANES, LANES), f32)],
        compiler_params=params(),
        name="pack",
    )(torque, contact, counts, init, mass)


def main_call(recv, par):
    tile = (PAD, LANES)
    scratch = [
        (CHUNKS * LANES, LANES),
        (DOF, *tile),
        (GROUP, DOF, *tile),
        (3, 72, 2 * PAD, LANES),
        (18, 2 * PAD, LANES),
        (HS, BLOCKS, *tile),
        (HS, BLOCKS, *tile),
        (HS, BLOCKS, *tile),
        (STEPS, *tile),
        (STEPS, *tile),
        (GROUP, 2 * PAD, LANES),
        (GROUP, 2 * PAD, LANES),
        (GROUP, 2 * PAD, LANES),
        (1, 2 * PAD, LANES),
        (BLOCKS, *tile),
        (BLOCKS, *tile),
        (BLOCKS, *tile),
        (2 * PAD, LANES),
        (8, LANES),
    ]
    return pl.pallas_call(
        main_kernel,
        out_shape=jax.ShapeDtypeStruct((LANES, OUT_CHUNKS, LANES), f32),
        scratch_shapes=[pltpu.VMEM(shape, f32) for shape in scratch],
        compiler_params=params(),
        name="parareal",
    )(recv, par)


def unpack_call(core, recv):
    half = jax.ShapeDtypeStruct((2, 2 * DOF, LANES), f32)
    return pl.pallas_call(
        unpack_kernel,
        in_specs=[pl.BlockSpec(memory_space=pltpu.SMEM), pl.BlockSpec(memory_space=pltpu.VMEM)],
        out_shape=(half, half, jax.ShapeDtypeStruct((8, LANES), f32)),
        scratch_shapes=[pltpu.VMEM((OUT_CHUNKS * LANES, LANES), f32)],
        compiler_params=params(),
        name="unpack",
    )(core, recv)


def param_table(*vectors):
    table = jnp.stack([jnp.pad(v, (0, PAD - DOF)) for v in vectors], axis=1)
    return jnp.pad(table, ((0, 0), (0, 8 - len(vectors))))


def swapped(value):
    return lax.ppermute(value, "c", [(0, 1), (1, 0)])


def exchanged(value):
    return lax.all_to_all(value, PEERS, split_axis=0, concat_axis=0, tiled=True)


def shards(init_state, torque, contact, mass_inverse, *vectors):
    core = lax.axis_index("c")
    block = lax.axis_index("y")
    is_low = core == 0
    contact_f = contact.astype(f32)
    counts = jnp.sum(contact_f, axis=1, keepdims=True)

    def half(value, which):
        return lax.dynamic_slice_in_dim(value, which * LANES, LANES, value.ndim - 1)

    mass_here = lax.dynamic_index_in_dim(mass_inverse, block % 2, 0, keepdims=False)
    mass_here = jnp.pad(mass_here, ((0, 0), (0, PAD - DOF)))
    mass_here = jnp.pad(mass_here.reshape(DOF * PAD), (0, 12 * LANES - DOF * PAD)).reshape(12, LANES)
    small = jnp.concatenate(
        [half(contact_f, 1 - core), jnp.broadcast_to(counts, (4, LANES)), mass_here], axis=0
    )
    small_back = swapped(small)
    torque_back = swapped(half(torque, 1 - core))

    def in_order(own, back):
        return jnp.where(is_low, jnp.concatenate([own, back]), jnp.concatenate([back, own]))

    torque_all = in_order(half(torque, core), torque_back)
    contact_all = in_order(half(contact_f, core), small_back[0:4])
    counts_all = in_order(counts, small_back[4:8, 0:1])
    mass_sent = jnp.where(block // 2 == core, mass_here, small_back[8:20])

    sent = pack_call(torque_all, contact_all, counts_all, half(init_state, core), mass_sent)
    solved = main_call(exchanged(sent), param_table(*vectors))
    mine, other, corr = unpack_call(core[None].astype(jnp.int32), exchanged(solved))
    back, corr_back = swapped(other), swapped(corr)

    def side_by_side(own, back):
        return jnp.where(
            is_low, jnp.concatenate([own, back], axis=-1), jnp.concatenate([back, own], axis=-1)
        )

    return side_by_side(mine, back), side_by_side(corr, corr_back)[:ITERS]


def solution(mesh):
    torus = Mesh(mesh.devices.reshape(4, 8, 2, mesh.shape["env"]), ("x", "z", "c", "y"))
    return jax.shard_map(
        shards,
        mesh=torus,
        in_specs=(P(None, "y"), P(TM, None, "y"), P(TM, "y"), P(TM, None, None), P(), P(), P(), P(), P()),
        out_specs=(P(TM, None, "y"), P(None, "y")),
        check_vma=False,
    )
```

time: 368 us -> 183 us (0.50); the launches traced: 363 us -> 183 us
  blocking collectives: 196 us -> 19.9 us
  matrix products: 122 us -> 0 us
  Pallas kernels: 0 us -> 101 us
  waiting for transfers between devices: 12.8 us -> 29.6 us
  other arithmetic: 1.97 us -> 6.45 us
    all_gather x15 -> x0, blocking collectives: 196 us -> none  [prefix_by_axis(): pieces = jax.tree.map(lambda part: lax.all_gather(part, axis), running)]
    dot_general x291 -> x0, matrix products: 122 us -> none  [the longest x288 121 us: exact_dot(): jnp.dot(left, right, precision=lax.Precision.HIGHEST, preferred_element_t...]
    pallas_call x0 -> x3, Pallas kernels: none -> 101 us  [the longest x1 95.9 us: main_call(): pl.pallas_call(main_kernel, out_shape=jax.ShapeDtypeStruct((LANES, OUT_CH...]
    all_to_all x0 -> x1, blocking collectives: none -> 19.9 us  [exchanged(): return lax.all_to_all(value, PEERS, split_axis=0, concat_axis=0, tiled=True)]
    all_to_all x2 -> x1, waiting for transfers between devices: 12.8 us -> 28.6 us  [exchanged(): return lax.all_to_all(value, PEERS, split_axis=0, concat_axis=0, tiled=True)]
    all_to_all x2 -> x1, starting transfers between devices: 21.7 us -> 13.9 us  [exchanged(): return lax.all_to_all(value, PEERS, split_axis=0, concat_axis=0, tiled=True)]
    ppermute x0 -> x4, starting transfers between devices: none -> 6.56 us  [swapped(): return lax.ppermute(value, 'c', [(0, 1), (1, 0)])]
    select_n x0 -> x6, other arithmetic: none -> 4.81 us  [the longest x2 2.32 us: side_by_side(): jnp.where(is_low, jnp.concatenate([own, back], axis=-1), jnp.concatenate(...]
  transfers between devices with their start and end apart: 2 -> 5, of which waited for: 2 -> 2; matrix products, arithmetic and copies ran while one was open for 0% -> 3% of each run, Pallas kernels for 0% -> 0%
where the time goes in v1:
time: 183 us
  Pallas kernels  101 us (55%)
  waiting for transfers between devices  29.6 us (16%)
  starting transfers between devices  20.5 us (11%)
  blocking collectives  19.9 us (11%)
  other arithmetic  6.45 us (4%)
  local copies, waits for them, and re-layouts  4.75 us (3%)
    pallas_call x1, Pallas kernels, main_call(): pl.pallas_call(main_kernel, out_shape=jax.ShapeDtypeStruct((LANES, OUT_CH...  95.9 us
    all_to_all x1, waiting for transfers between devices, exchanged(): return lax.all_to_all(value, PEERS, split_axis=0, concat_axis=0, tiled=True)  28.6 us
    all_to_all x1, blocking collectives, exchanged(): return lax.all_to_all(value, PEERS, split_axis=0, concat_axis=0, tiled=True)  19.9 us
    all_to_all x1, starting transfers between devices, exchanged(): return lax.all_to_all(value, PEERS, split_axis=0, concat_axis=0, tiled=True)  13.9 us
    ppermute x4, starting transfers between devices, swapped(): return lax.ppermute(value, 'c', [(0, 1), (1, 0)])  6.56 us
  transfers between devices with their start and end apart: 5, of which 2 were waited for; matrix products, arithmetic and copies ran while one was open for 3% of the time, Pallas kernels for 0%

profile of v1, /device:TPU:1, one launch (start us, length us, event | category | flops | bytes accessed | tf_op | source)
XLA Modules:
  0.0 182.6 jit_solution(4616663284237107390)
XLA Ops:
  0.6 0.0 copy-start
  0.6 0.0 copy-start.3
  0.7 0.0 copy-start.2
  0.7 0.8 convert_element_type.15
  1.5 0.8 convert_reduce_fusion
  2.3 0.0 copy-done.3
  2.3 0.1 reshape.71
  2.4 0.1 pad.53.clone
  2.5 0.1 pad_maximum_fusion
  2.6 3.2 %collective-permute-start.1 = (f32[20,128]{1,0:T(8,128)S(1)}, f32[20,128]{1,0:T(8,128)S(1)}, u32[]{:S(2)}, u32[]{:S(2)}) collective-permute-start(f32[20,128]{1,0:T(8,128)S(1)} %pad_maximum_fusion), channel_id=1, source_target_pairs={{0,4},{4,0},{1,5},{5,1},{2,6},{6,2},{3,7},{7,3},{8,12},{12,8},{9,1... | collective-permute-start | bytes 30728 | tf_op jit(solution)/shard_map/ppermute | solution.py:370
  5.8 0.0 copy-done.2
  5.8 0.1 collective-permute-start
  6.0 0.0 copy-done
  6.0 0.6 constant_dynamic-slice_fusion.init
  6.6 0.1 copy.44
  6.7 0.0 collective-permute-done.1
  6.7 0.6 maximum_select_fusion.2.contact
  7.3 0.6 slice_select_fusion.mass
  7.9 0.6 maximum_select_fusion.3.counts
  8.5 0.0 collective-permute-done
  8.5 0.7 maximum_select_fusion.torque
  9.2 2.8 %pack.1 = f32[128,16,128]{2,1,0:T(8,128)} custom-call(f32[8,35,128]{2,1,0:T(8,128)} %maximum_select_fusion.torque, f32[8,128]{1,0:T(8,128)} %maximum_select_fusion.2.contact, f32[8,1]{1,0:T(8,128)} %maximum_select_fusion.3.counts, f32[70,128]{1,0:T(8,128)} %constant_dynamic-slice_fusion.init, f32[12,128]{1,0:T(8,128)} %slice_select_fusion.mass), custom_call_target="tpu_custom_call" | custom-call | tf_op jit(solution)/shard_map/pack/pallas_call | solution.py:311
  12.0 0.0 copy-start.8
  12.0 13.9 %all-to-all-start = ((f32[128,16,128]{2,1,0:T(8,128)}), f32[128,16,128]{2,1,0:T(8,128)S(1)}, u32[]{:S(2)}, u32[]{:S(2)}) async-start(f32[128,16,128]{2,1,0:T(8,128)} %pack.1), calls=%async_computation | async-start | bytes 2097152 | tf_op jit(solution)/shard_map/all_to_all | solution.py:374
  25.9 0.0 copy-done.8
  25.9 0.0 copy-start.4
  25.9 0.0 copy-start.5
  26.0 0.6 copy-done.4
  26.6 0.0 copy-done.5
  26.6 0.0 copy-start.6
  26.6 0.0 copy-start.7
  26.6 0.6 copy-done.6
  27.3 0.0 copy-done.7
  27.3 0.1 copy.46
  27.4 0.6 pad.35.par
  28.0 28.6 %all-to-all-done.recv = f32[128,16,128]{2,1,0:T(8,128)S(1)} async-done(((f32[128,16,128]{2,1,0:T(8,128)}), f32[128,16,128]{2,1,0:T(8,128)S(1)}, u32[]{:S(2)}, u32[]{:S(2)}) %all-to-all-start) | async-done | bytes 1048608 | tf_op jit(solution)/shard_map/all_to_all | solution.py:374
  56.6 0.0 copy-start.1
  56.6 1.0 copy-done.1
  57.6 95.9 %parareal.1 = f32[128,4,128]{2,1,0:T(4,128)} custom-call(f32[128,16,128]{2,1,0:T(8,128)} %copy-done.1, f32[40,8]{1,0:T(8,128)} %pad.35.par), custom_call_target="tpu_custom_call" | custom-call | tf_op jit(solution)/shard_map/parareal/pallas_call | solution.py:343
  153.5 19.9 %all_to_all.10.recv = f32[128,4,128]{2,1,0:T(4,128)} all-to-all(f32[128,4,128]{2,1,0:T(4,128)} %parareal.1), channel_id=1, replica_groups=mesh['x'=4,'z'=8,'c'=2,'y'=4] {'y','x','z'}, dimensions={0} | all-to-all | bytes 524288 | tf_op jit(solution)/shard_map/all_to_all | solution.py:374
  173.4 1.8 %unpack.1 = (f32[2,70,128]{2,1,0:T(8,128)}, f32[2,70,128]{2,1,0:T(8,128)}, f32[8,128]{1,0:T(8,128)}) custom-call(s32[1]{0:T(128)} %bitcast.core, f32[128,4,128]{2,1,0:T(4,128)} %all_to_all.10.recv), custom_call_target="tpu_custom_call" | custom-call | tf_op jit(solution)/shard_map/unpack/pallas_call | solution.py:354
  175.2 3.2 %collective-permute-start.3 = (f32[8,128]{1,0:T(8,128)}, f32[8,128]{1,0:T(8,128)S(1)}, u32[]{:S(2)}, u32[]{:S(2)}) collective-permute-start(f32[8,128]{1,0:T(8,128)} %get-tuple-element.7), channel_id=1, source_target_pairs={{0,4},{4,0},{1,5},{5,1},{2,6},{6,2},{3,7},{7,3},{8,12},{12,8},{9,1... | collective-permute-start | bytes 12296 | tf_op jit(solution)/shard_map/ppermute | solution.py:370
  178.5 0.0 collective-permute-start.2
  178.5 1.0 collective-permute-done.3
  179.5 1.3 fusion
  180.8 0.0 collective-permute-done.2
  180.8 1.0 maximum_select_fusion.1
  181.8 0.7 copy.47
  (14 shorter events, 0.1 us)
Async XLA Ops:
  0.6 5.3 %copy-start = (f32[70,256]{1,0:T(8,128)S(1)}, f32[70,256]{1,0:T(8,128)}, u32[]{:S(2)}) copy-start(f32[70,256]{1,0:T(8,128)} %param.9) | copy-start | bytes 215044
  0.6 1.6 copy-start.3
  0.7 5.1 %copy-start.2 = (f32[4,35,256]{2,0,1:T(4,128)S(1)}, f32[4,35,256]{2,0,1:T(4,128)}, u32[]{:S(2)}) copy-start(f32[4,35,256]{2,0,1:T(4,128)} %param.10) | copy-start | bytes 430084
  2.6 4.1 %collective-permute-start.1 = (f32[20,128]{1,0:T(8,128)S(1)}, f32[20,128]{1,0:T(8,128)S(1)}, u32[]{:S(2)}, u32[]{:S(2)}) collective-permute-start(f32[20,128]{1,0:T(8,128)S(1)} %pad_maximum_fusion), channel_id=1, source_target_pairs={{0,4},{4,0},{1,5},{5,1},{2,6},{6,2},{3,7},{7,3},{8,12},{12,8},{9,1... | collective-permute-start | bytes 30728 | tf_op jit(solution)/shard_map/ppermute | solution.py:370
  5.8 2.7 %collective-permute-start = (f32[4,35,128]{2,1,0:T(8,128)S(1)}, f32[4,35,128]{2,1,0:T(8,128)S(1)}, u32[]{:S(2)}, u32[]{:S(2)}) collective-permute-start(f32[4,35,128]{2,1,0:T(8,128)S(1)} %copy.49), channel_id=1, source_target_pairs={{0,4},{4,0},{1,5},{5,1},{2,6},{6,2},{3,7},{7,3},{8,12},{12,8},{9,1... | collective-permute-start | bytes 215048 | tf_op jit(solution)/shard_map/ppermute | solution.py:370
  12.0 13.9 %copy-start.8 = (f32[35]{0:T(128)S(1)}, f32[35]{0:T(128)}, u32[]{:S(2)}) copy-start(f32[35]{0:T(128)} %param.13) | copy-start | bytes 424
  12.0 44.6 %all-to-all-start = ((f32[128,16,128]{2,1,0:T(8,128)}), f32[128,16,128]{2,1,0:T(8,128)S(1)}, u32[]{:S(2)}, u32[]{:S(2)}) async-start(f32[128,16,128]{2,1,0:T(8,128)} %pack.1), calls=%async_computation | async-start | bytes 2097152 | tf_op jit(solution)/shard_map/all_to_all | solution.py:374
  25.9 0.7 copy-start.4
  25.9 0.7 copy-start.5
  26.6 0.7 copy-start.6
  26.6 0.7 copy-start.7
  56.6 1.0 copy-start.1
  175.2 4.2 %collective-permute-start.3 = (f32[8,128]{1,0:T(8,128)}, f32[8,128]{1,0:T(8,128)S(1)}, u32[]{:S(2)}, u32[]{:S(2)}) collective-permute-start(f32[8,128]{1,0:T(8,128)} %get-tuple-element.7), channel_id=1, source_target_pairs={{0,4},{4,0},{1,5},{5,1},{2,6},{6,2},{3,7},{7,3},{8,12},{12,8},{9,1... | collective-permute-start | bytes 12296 | tf_op jit(solution)/shard_map/ppermute | solution.py:370
  178.5 2.4 %collective-permute-start.2 = (f32[2,70,128]{2,1,0:T(8,128)}, f32[2,70,128]{2,1,0:T(8,128)S(1)}, u32[]{:S(2)}, u32[]{:S(2)}) collective-permute-start(f32[2,70,128]{2,1,0:T(8,128)} %get-tuple-element.6), channel_id=1, source_target_pairs={{0,4},{4,0},{1,5},{5,1},{2,6},{6,2},{3,7},{7,3},{8,12},{12,8},{9,1... | collective-permute-start | bytes 215048 | tf_op jit(solution)/shard_map/ppermute | solution.py:370

commit v2 on v1

--- a/solution.py
+++ b/solution.py
@@ -21,7 +21,7 @@
 LANES = 128
 ENV = 1024
 TM = ("x", "z", "c")
-PEERS = ("y", "x", "z")
+PEERS = ("x", "z")
 
 DT = 0.05
 FINE = DT / SUB
@@ -30,11 +30,14 @@
 
 ROW_CONTACT = STEPS * PAD
 ROW_COUNT = ROW_CONTACT + 8
-ROW_INIT = ROW_COUNT + 8
-ROW_MASS = 512
-CHUNKS = 16
-OUT_CHUNKS = 4
-VMEM_LIMIT = 56 * 1024 * 1024
+ROW_TAIL = ROW_COUNT + 8
+IN_ROWS = 12
+FOLD_ROWS = 18
+FOLD_COLS = 36
+FOLD = FOLD_ROWS * FOLD_COLS
+MASS_ROWS = 5
+CHUNKS = IN_ROWS + GROUP * MASS_ROWS
+VMEM_LIMIT = 24 * 1024 * 1024
 
 f32 = jnp.float32
 
@@ -73,18 +76,52 @@
     return jnp.where(group >= by, pltpu.roll(value, by, 1), 0.0)
 
 
-def pack_kernel(torque, contact, counts, init, mass, out, rows):
+def fold_index(k, i):
+    k, i = min(k, i), max(k, i)
+    if k < FOLD_ROWS:
+        return k * FOLD_COLS + i + 1
+    return (DOF - 1 - k) * FOLD_COLS + DOF - 1 - i
+
+
+def half_of(which):
+    return pl.ds(pl.multiple_of(which * LANES, LANES), LANES)
+
+
+def split_kernel(core, torque, contact, send, counts):
+    there = half_of(1 - core[0])
+    send[...] = jnp.zeros_like(send)
+    for t in range(4):
+        send[t * PAD : t * PAD + DOF, :] = torque[:, t, there]
+    send[4 * PAD : 4 * PAD + 4, :] = contact[:, there].astype(f32)
+    total = jnp.sum(contact[...].astype(f32), axis=1, keepdims=True)
+    for peer in range(8):
+        counts[peer] = jnp.broadcast_to(total, (4, LANES))
+
+
+def pack_kernel(core, torque, contact, back, totals, mass, tails, out, rows):
+    me = core[0]
+    here = half_of(me)
     rows[...] = jnp.zeros_like(rows)
-    for t in range(STEPS):
-        rows[t * PAD : t * PAD + DOF, :] = torque[t]
-    rows[ROW_CONTACT : ROW_CONTACT + 8, :] = contact[...]
-    rows[ROW_COUNT : ROW_COUNT + 8, :] = jnp.broadcast_to(counts[...], (8, LANES))
-    rows[ROW_INIT : ROW_INIT + DOF, :] = init[:DOF, :]
-    rows[ROW_INIT + PAD : ROW_INIT + PAD + DOF, :] = init[DOF:, :]
-    for c in range(4):
-        out[:, c, :] = rows[c * LANES : (c + 1) * LANES, :].T
-    for c in range(4, CHUNKS):
-        out[:, c, :] = jnp.broadcast_to(mass[c - 4 : c - 3, :], (LANES, LANES))
+    for t in range(4):
+        rows[pl.ds(pl.multiple_of((4 * me + t) * PAD, 8), DOF), :] = torque[:, t, here]
+        rows[pl.ds(pl.multiple_of((4 * (1 - me) + t) * PAD, 8), PAD), :] = back[t * PAD : (t + 1) * PAD, :]
+    own = contact[:, here].astype(f32)
+    other = back[4 * PAD : 4 * PAD + 4, :]
+    rows[ROW_CONTACT : ROW_CONTACT + 8, :] = jnp.where(
+        me == 0, jnp.concatenate([own, other]), jnp.concatenate([other, own])
+    )
+    rows[ROW_COUNT : ROW_COUNT + 8, :] = totals[...]
+    block = lane_index(8) >> 5
+    tail = jnp.zeros((8, LANES), f32)
+    for b in range(GROUP):
+        tail = jnp.where(block == b, tails[:, b : b + 1], tail)
+    rows[ROW_TAIL : ROW_TAIL + 8, :] = tail
+    for c in range(3):
+        turned = rows[c * LANES : (c + 1) * LANES, :].T
+        for e in range(BLOCKS):
+            out[:, e * 3 + c, :] = turned[e * CHIPS : (e + 1) * CHIPS]
+    for m in range(GROUP * MASS_ROWS):
+        out[:, IN_ROWS + m, :] = jnp.broadcast_to(mass[m : m + 1, :], (CHIPS, LANES))
 
 
 def state_row(k):
@@ -92,31 +129,37 @@
 
 
 def main_kernel(
-    recv, par, out, rows, mb, ma, wide, cols, tau_b, stiff_b, damp_b, spring, fric, start, end, shift, diff, pos, vel, force, vec, corr
+    chip, init_ref, recv, par, out, rows, fold, mb, ma, wide, cols, tau_b, stiff_b, damp_b, spring, fric, start, end, shift, diff, pos, vel, force, vec, corr
 ):
-    for c in range(CHUNKS - 1):
-        rows[c * LANES : (c + 1) * LANES, :] = recv[:, c, :].T
+    for c in range(3):
+        rows[c * LANES : (c + 1) * LANES, :] = jnp.concatenate(
+            [recv[:, e * 3 + c, :] for e in range(BLOCKS)]
+        ).T
+    for m in range(MASS_ROWS):
+        fold[m * LANES : (m + 1) * LANES, :] = jnp.concatenate(
+            [recv[:, IN_ROWS + b * MASS_ROWS + m, :] for b in range(GROUP)]
+        ).T
+    fold[MASS_ROWS * LANES : FOLD, :] = rows[ROW_TAIL : ROW_TAIL + 8, :]
 
     def param(i):
         return jnp.broadcast_to(par[:, i : i + 1], (PAD, LANES))
 
     stiffness, damping, gravity, contact_stiffness, contact_damping = (param(i) for i in range(5))
 
-    mb[...] = jnp.zeros_like(mb)
-    ma[...] = jnp.zeros_like(ma)
+    for k in range(DOF):
+        for i in range(DOF):
+            at = fold_index(k, i)
+            mb[k, i : i + 1, :] = fold[at : at + 1, :]
+        mb[k, DOF:PAD, :] = jnp.zeros((PAD - DOF, LANES), f32)
 
     def place_mass(k, carry):
-        part = rows[pl.ds(pl.multiple_of(ROW_MASS + k * PAD, 8), PAD), :]
-        mb[k] = part
-        for b, spread in enumerate(block_spread(part)):
+        for b, spread in enumerate(block_spread(mb[k])):
             ma[b, k] = spread
         return carry
 
     lax.fori_loop(0, DOF, place_mass, 0)
 
-    count = rows[ROW_COUNT : ROW_COUNT + 8, :]
-    total = count + pltpu.roll(count, 32, 1) + pltpu.roll(count, 64, 1) + pltpu.roll(count, 96, 1)
-    mean = total / ENV
+    mean = rows[ROW_COUNT : ROW_COUNT + 8, :] / ENV
     for t in range(STEPS):
         here = mean[t : t + 1, :]
         spring[t] = (stiffness + gravity + here * contact_stiffness) * (FINE * DT)
@@ -201,8 +244,11 @@
         return lax.fori_loop(0, 7, more, value)
 
     first = (lane_index(2 * PAD) & 31) == 0
-    init = jnp.where(first, rows[ROW_INIT : ROW_INIT + 2 * PAD, :], 0.0)
-    init = jnp.concatenate([init[:PAD] * TURN, init[PAD:] * (FINE * TURN)], axis=0)
+    back_by = LANES - chip[0]
+    vec[...] = jnp.zeros_like(vec)
+    vec[0:DOF, :] = init_ref[:DOF, half_of(chip[1])] * TURN
+    vec[PAD : PAD + DOF, :] = init_ref[DOF:, half_of(chip[1])] * (FINE * TURN)
+    init = jnp.where(first, pltpu.roll(vec[...], back_by, 1), 0.0)
 
     def driven_slice(b, qw):
         return slice_step(b, qw[0], qw[1], True)
@@ -281,46 +327,59 @@
 
     lax.fori_loop(0, ITERS, iteration, 0)
 
-    rows[0 : OUT_CHUNKS * LANES, :] = jnp.zeros((OUT_CHUNKS * LANES, LANES), f32)
     for b in range(GROUP):
         rows[b * 2 * PAD : b * 2 * PAD + PAD, :] = end[b, :PAD, :] * (1.0 / TURN)
         rows[b * 2 * PAD + PAD : (b + 1) * 2 * PAD, :] = end[b, PAD:, :] * (1.0 / (TURN * FINE))
     rows[GROUP * 2 * PAD : GROUP * 2 * PAD + 8, :] = corr[...]
-    for c in range(OUT_CHUNKS):
-        out[:, c, :] = rows[c * LANES : (c + 1) * LANES, :].T
-
-
-def unpack_kernel(core, recv, mine, other, corr, rows):
-    for c in range(OUT_CHUNKS):
-        rows[c * LANES : (c + 1) * LANES, :] = recv[:, c, :].T
-    here = core[0] * 2
-    for ref, base in ((mine, here), (other, 2 - here)):
+    for c in range(3):
+        turned = rows[c * LANES : (c + 1) * LANES, :].T
+        for e in range(BLOCKS):
+            at = e * 3 + c
+            out[:, at // 4, at % 4, :] = turned[e * CHIPS : (e + 1) * CHIPS]
+
+
+def unpack_kernel(core, recv, mine, send, rows):
+    for c in range(3):
+        at = [e * 3 + c for e in range(BLOCKS)]
+        rows[c * LANES : (c + 1) * LANES, :] = jnp.concatenate([recv[:, i // 4, i % 4, :] for i in at]).T
+    corr = rows[GROUP * 2 * PAD : GROUP * 2 * PAD + 8, :]
+    for ref, which in ((mine, core[0]), (send, 1 - core[0])):
+        ref[0 : 4 * PAD, :] = rows[pl.ds(pl.multiple_of(which * 4 * PAD, 8), 4 * PAD), :]
+        ref[4 * PAD :, :] = corr
+
+
+def join_kernel(core, mine, back, out, corr):
+    for ref, which in ((mine, core[0]), (back, 1 - core[0])):
+        part = half_of(which)
         for s in range(2):
-            at = pl.multiple_of((base + s) * 2 * PAD, 8)
-            whole = rows[pl.ds(at, 2 * PAD), :]
-            ref[s, 0:DOF, :] = whole[:DOF]
-            ref[s, DOF : 2 * DOF, :] = whole[PAD : PAD + DOF]
-    corr[...] = rows[GROUP * 2 * PAD : GROUP * 2 * PAD + 8, :]
-
-
-def params(**more):
-    return pltpu.CompilerParams(vmem_limit_bytes=VMEM_LIMIT, **more)
-
-
-def pack_call(torque, contact, counts, init, mass):
+            out[0:DOF, s, part] = ref[s * 2 * PAD : s * 2 * PAD + DOF, :]
+            out[DOF : 2 * DOF, s, part] = ref[s * 2 * PAD + PAD : s * 2 * PAD + PAD + DOF, :]
+        corr[:, part] = ref[4 * PAD : 4 * PAD + ITERS, :]
+
+
+SWAP = (4 * PAD + 8, LANES)
+
+
+def local_call(kernel, name, out_shapes, scratch, scalars, *arrays):
+    smem = pl.BlockSpec(memory_space=pltpu.SMEM)
+    vmem = pl.BlockSpec(memory_space=pltpu.VMEM)
+    shapes = tuple(jax.ShapeDtypeStruct(shape, f32) for shape in out_shapes)
     return pl.pallas_call(
-        pack_kernel,
-        out_shape=jax.ShapeDtypeStruct((LANES, CHUNKS, LANES), f32),
-        scratch_shapes=[pltpu.VMEM((4 * LANES, LANES), f32)],
-        compiler_params=params(),
-        name="pack",
-    )(torque, contact, counts, init, mass)
-
-
-def main_call(recv, par):
+        kernel,
+        in_specs=[smem] + [vmem] * len(arrays),
+        out_specs=tuple(vmem for _ in shapes) if len(shapes) > 1 else vmem,
+        out_shape=shapes if len(shapes) > 1 else shapes[0],
+        scratch_shapes=[pltpu.VMEM(shape, f32) for shape in scratch],
+        compiler_params=pltpu.CompilerParams(vmem_limit_bytes=VMEM_LIMIT),
+        name=name,
+    )(scalars, *arrays)
+
+
+def main_call(chip, init, recv, par):
     tile = (PAD, LANES)
     scratch = [
-        (CHUNKS * LANES, LANES),
+        (3 * LANES, LANES),
+        (FOLD, LANES),
         (DOF, *tile),
         (GROUP, DOF, *tile),
         (3, 72, 2 * PAD, LANES),
@@ -340,25 +399,7 @@
         (2 * PAD, LANES),
         (8, LANES),
     ]
-    return pl.pallas_call(
-        main_kernel,
-        out_shape=jax.ShapeDtypeStruct((LANES, OUT_CHUNKS, LANES), f32),
-        scratch_shapes=[pltpu.VMEM(shape, f32) for shape in scratch],
-        compiler_params=params(),
-        name="parareal",
-    )(recv, par)
-
-
-def unpack_call(core, recv):
-    half = jax.ShapeDtypeStruct((2, 2 * DOF, LANES), f32)
-    return pl.pallas_call(
-        unpack_kernel,
-        in_specs=[pl.BlockSpec(memory_space=pltpu.SMEM), pl.BlockSpec(memory_space=pltpu.VMEM)],
-        out_shape=(half, half, jax.ShapeDtypeStruct((8, LANES), f32)),
-        scratch_shapes=[pltpu.VMEM((OUT_CHUNKS * LANES, LANES), f32)],
-        compiler_params=params(),
-        name="unpack",
-    )(core, recv)
+    return local_call(main_kernel, "parareal", [(CHIPS, 3, 4, LANES)], scratch, chip, init, recv, par)
 
 
 def param_table(*vectors):
@@ -374,44 +415,56 @@
     return lax.all_to_all(value, PEERS, split_axis=0, concat_axis=0, tiled=True)
 
 
+def folded(matrices):
+    row = lax.broadcasted_iota(jnp.int32, (FOLD_ROWS, FOLD_COLS), 0)
+    col = lax.broadcasted_iota(jnp.int32, (FOLD_ROWS, FOLD_COLS), 1)
+    plain = jnp.pad(matrices, ((0, 0), (0, 0), (1, 0)))[:, :FOLD_ROWS]
+    turned = jnp.pad(matrices[:, ::-1, ::-1], ((0, 0), (0, 0), (0, 1)))[:, :FOLD_ROWS]
+    return jnp.where(col <= row, turned, plain).reshape(-1, FOLD)
+
+
 def shards(init_state, torque, contact, mass_inverse, *vectors):
-    core = lax.axis_index("c")
-    block = lax.axis_index("y")
-    is_low = core == 0
-    contact_f = contact.astype(f32)
-    counts = jnp.sum(contact_f, axis=1, keepdims=True)
-
-    def half(value, which):
-        return lax.dynamic_slice_in_dim(value, which * LANES, LANES, value.ndim - 1)
-
-    mass_here = lax.dynamic_index_in_dim(mass_inverse, block % 2, 0, keepdims=False)
-    mass_here = jnp.pad(mass_here, ((0, 0), (0, PAD - DOF)))
-    mass_here = jnp.pad(mass_here.reshape(DOF * PAD), (0, 12 * LANES - DOF * PAD)).reshape(12, LANES)
-    small = jnp.concatenate(
-        [half(contact_f, 1 - core), jnp.broadcast_to(counts, (4, LANES)), mass_here], axis=0
-    )
-    small_back = swapped(small)
-    torque_back = swapped(half(torque, 1 - core))
-
-    def in_order(own, back):
-        return jnp.where(is_low, jnp.concatenate([own, back]), jnp.concatenate([back, own]))
-
-    torque_all = in_order(half(torque, core), torque_back)
-    contact_all = in_order(half(contact_f, core), small_back[0:4])
-    counts_all = in_order(counts, small_back[4:8, 0:1])
-    mass_sent = jnp.where(block // 2 == core, mass_here, small_back[8:20])
-
-    sent = pack_call(torque_all, contact_all, counts_all, half(init_state, core), mass_sent)
-    solved = main_call(exchanged(sent), param_table(*vectors))
-    mine, other, corr = unpack_call(core[None].astype(jnp.int32), exchanged(solved))
-    back, corr_back = swapped(other), swapped(corr)
-
-    def side_by_side(own, back):
-        return jnp.where(
-            is_low, jnp.concatenate([own, back], axis=-1), jnp.concatenate([back, own], axis=-1)
+    core = lax.axis_index("c").astype(jnp.int32)
+    chip = (lax.axis_index("x") * lax.axis_size("z") + lax.axis_index("z")).astype(jnp.int32)
+
+    mass_back = swapped(mass_inverse)
+    torque = torque.transpose(1, 0, 2)
+    send, counts = local_call(split_kernel, "split", [SWAP, (8, 4, LANES)], [], core[None], torque, contact)
+    back = swapped(send)
+    counts = lax.all_to_all(counts, ("c", "y"), split_axis=0, concat_axis=0, tiled=True)
+    totals = counts.reshape(2, BLOCKS, 4, LANES).sum(axis=1).reshape(8, LANES)
+    order = core == 0
+    matrices = folded(
+        jnp.where(
+            order,
+            jnp.concatenate([mass_inverse, mass_back]),
+            jnp.concatenate([mass_back, mass_inverse]),
         )
-
-    return side_by_side(mine, back), side_by_side(corr, corr_back)[:ITERS]
+    )
+    mass_rows = matrices[:, : MASS_ROWS * LANES].reshape(GROUP * MASS_ROWS, LANES)
+    mass_tails = matrices[:, MASS_ROWS * LANES :].T
+
+    sent = local_call(
+        pack_kernel,
+        "pack",
+        [(CHIPS, CHUNKS, LANES)],
+        [(3 * LANES, LANES)],
+        core[None],
+        torque,
+        contact,
+        back,
+        totals,
+        mass_rows,
+        mass_tails,
+    )
+    solved = main_call(jnp.stack([chip, core]), init_state, exchanged(sent), param_table(*vectors))
+    mine, send = local_call(
+        unpack_kernel, "unpack", [SWAP, SWAP], [(3 * LANES, LANES)], core[None], exchanged(solved)
+    )
+    final, corr = local_call(
+        join_kernel, "join", [(2 * DOF, 2, 2 * LANES), (ITERS, 2 * LANES)], [], core[None], mine, swapped(send)
+    )
+    return final.transpose(1, 0, 2), corr
 
 
 def solution(mesh):

time: 183 us -> 158 us (0.86)
  waiting for transfers between devices: 29.6 us -> 17.9 us
  other arithmetic: 6.45 us -> 0.26 us
  Pallas kernels: 101 us -> 97.2 us
  blocking collectives: 19.9 us -> 17.3 us
    all_to_all x1, waiting for transfers between devices: 28.6 us -> 13.9 us  [exchanged(): return lax.all_to_all(value, PEERS, split_axis=0, concat_axis=0, tiled=True)]
    select_n x6 -> x2, other arithmetic: 4.81 us -> 0.17 us  [the longest x1 0.09 us: folded(): return jnp.where(col <= row, turned, plain).reshape(-1, FOLD)]
    all_to_all x0 -> x1, starting transfers between devices: none -> 3.75 us  [shards(): lax.all_to_all(counts, ('c', 'y'), split_axis=0, concat_axis=0, tiled=True)]
    pallas_call x3 -> x5, Pallas kernels: 101 us -> 97.2 us  [local_call(): pl.pallas_call(kernel, in_specs=[smem] + [vmem] * len(arrays), out_specs=...]
    all_to_all x1, starting transfers between devices: 13.9 us -> 10.7 us  [exchanged(): return lax.all_to_all(value, PEERS, split_axis=0, concat_axis=0, tiled=True)]
    all_to_all x0 -> x1, waiting for transfers between devices: none -> 3.05 us  [shards(): lax.all_to_all(counts, ('c', 'y'), split_axis=0, concat_axis=0, tiled=True)]
    all_to_all x1, blocking collectives: 19.9 us -> 17.3 us  [exchanged(): return lax.all_to_all(value, PEERS, split_axis=0, concat_axis=0, tiled=True)]
    ppermute x4 -> x3, starting transfers between devices: 6.56 us -> 6.24 us  [swapped(): return lax.ppermute(value, 'c', [(0, 1), (1, 0)])]
  transfers between devices with their start and end apart: 5 -> 5, of which waited for: 2 -> 3; matrix products, arithmetic and copies ran while one was open for 3% -> 0% of each run, Pallas kernels for 0% -> 0%
where the time goes in v2:
time: 158 us; the launch traced here: 157 us
  Pallas kernels  97.2 us (62%)
  starting transfers between devices  20.7 us (13%)
  waiting for transfers between devices  17.9 us (11%)
  blocking collectives  17.3 us (11%)
  local copies, waits for them, and re-layouts  3.35 us (2%)
    pallas_call x5, Pallas kernels, local_call(): pl.pallas_call(kernel, in_specs=[smem] + [vmem] * len(arrays), out_specs=...  97.2 us
    all_to_all x1, blocking collectives, exchanged(): return lax.all_to_all(value, PEERS, split_axis=0, concat_axis=0, tiled=True)  17.3 us
    all_to_all x1, waiting for transfers between devices, exchanged(): return lax.all_to_all(value, PEERS, split_axis=0, concat_axis=0, tiled=True)  13.9 us
    all_to_all x1, starting transfers between devices, exchanged(): return lax.all_to_all(value, PEERS, split_axis=0, concat_axis=0, tiled=True)  10.7 us
    ppermute x3, starting transfers between devices, swapped(): return lax.ppermute(value, 'c', [(0, 1), (1, 0)])  6.24 us
    all_to_all x1, starting transfers between devices, shards(): lax.all_to_all(counts, ('c', 'y'), split_axis=0, concat_axis=0, tiled=True)  3.75 us
  transfers between devices with their start and end apart: 5, of which 3 were waited for; matrix products, arithmetic and copies ran while one was open for 0% of the time, Pallas kernels for 0%

profile of v2, /device:TPU:1, one launch (start us, length us, event | category | flops | bytes accessed | tf_op | source)
XLA Modules:
  0.0 157.5 jit_solution(9718147819161099319)
XLA Ops:
  0.6 3.3 %collective-permute-start.1 = (f32[2,35,35]{2,0,1:T(2,128)}, f32[2,35,35]{2,0,1:T(2,128)S(1)}, u32[]{:S(2)}, u32[]{:S(2)}) collective-permute-start(f32[2,35,35]{2,0,1:T(2,128)} %param.12), channel_id=1, source_target_pairs={{0,4},{4,0},{1,5},{5,1},{2,6},{6,2},{3,7},{7,3},{8,12},{12,8},{9,1... | collective-permute-start | bytes 29408 | tf_op jit(solution)/shard_map/ppermute | solution.py:411
  3.9 0.0 copy-start.3
  3.9 0.7 copy-done.3
  4.6 0.0 copy-start
  4.6 0.9 copy-done
  5.5 0.7 split.1
  6.2 0.0 copy-start.5
  6.2 0.0 collective-permute-start
  6.3 3.7 %all-to-all-start = ((f32[8,4,128]{2,1,0:T(4,128)}), f32[8,4,128]{2,1,0:T(4,128)S(1)}, u32[]{:S(2)}, u32[]{:S(2)}) async-start(f32[8,4,128]{2,1,0:T(4,128)} %get-tuple-element.9), calls=%async_computation | async-start | bytes 32768 | tf_op jit(solution)/shard_map/all_to_all | solution.py:434
  10.0 0.0 collective-permute-done.1
  10.0 0.0 copy-done.5
  10.0 0.1 maximum_select_fusion
  10.1 0.1 rev.3
  10.3 0.1 fusion
  10.4 0.0 copy-start.1
  10.4 0.1 reshape.18
  10.5 0.0 copy-start.4
  10.5 0.6 copy-done.4
  11.1 0.0 slice-start
  11.1 0.7 slice-done
  11.8 0.1 copy.27
  11.9 3.0 %all-to-all-done = f32[8,4,128]{2,1,0:T(4,128)S(1)} async-done(((f32[8,4,128]{2,1,0:T(4,128)}), f32[8,4,128]{2,1,0:T(4,128)S(1)}, u32[]{:S(2)}, u32[]{:S(2)}) %all-to-all-start) | async-done | bytes 16416 | tf_op jit(solution)/shard_map/all_to_all | solution.py:434
  14.9 0.0 collective-permute-done.back
  14.9 0.0 copy-done.1
  14.9 1.3 pack.1
  16.3 0.0 copy-start.10
  16.3 0.0 copy-start.6
  16.3 0.0 copy-start.7
  16.3 0.0 copy-start.8
  16.3 0.0 copy-start.9
  16.3 10.7 %all-to-all-start.1 = ((f32[32,32,128]{2,1,0:T(8,128)}), f32[32,32,128]{2,1,0:T(8,128)S(1)}, u32[]{:S(2)}, u32[]{:S(2)}) async-start(f32[32,32,128]{2,1,0:T(8,128)} %pack.1), calls=%async_computation.1 | async-start | bytes 1048576 | tf_op jit(solution)/shard_map/all_to_all | solution.py:415
  27.0 0.0 copy-start.2
  27.0 0.0 copy-done.10
  27.0 0.0 copy-done.6
  27.0 0.0 copy-done.7
  27.1 0.0 copy-done.8
  27.1 0.0 copy-done.9
  27.1 0.1 copy.26
  27.2 0.1 pad_add_fusion.chip
  27.3 13.9 %all-to-all-done.1.recv = f32[32,32,128]{2,1,0:T(8,128)S(1)} async-done(((f32[32,32,128]{2,1,0:T(8,128)}), f32[32,32,128]{2,1,0:T(8,128)S(1)}, u32[]{:S(2)}, u32[]{:S(2)}) %all-to-all-start.1) | async-done | bytes 524320 | tf_op jit(solution)/shard_map/all_to_all | solution.py:415
  41.2 0.0 copy-done.2
  41.2 94.2 %parareal.1 = f32[32,3,4,128]{3,2,1,0:T(4,128)S(1)} custom-call(s32[2]{0:T(128)S(1)} %pad_add_fusion.chip, f32[70,256]{1,0:T(8,128)S(1)} %copy-done.2, f32[32,32,128]{2,1,0:T(8,128)S(1)} %all-to-all-done.1.recv, f32[40,8]{1,0:T(8,128)S(1)} %pad.35.par), custom_call_target="tpu_custom_call" | custom-call | tf_op jit(solution)/shard_map/parareal/pallas_call | solution.py:367
  135.4 17.3 %all_to_all.15.recv = f32[32,3,4,128]{3,2,1,0:T(4,128)S(1)} all-to-all(f32[32,3,4,128]{3,2,1,0:T(4,128)S(1)} %parareal.1), channel_id=1, replica_groups=mesh['x'=4,'z'=8,'c'=2,'y'=4] {'x','z'}, dimensions={0} | all-to-all | bytes 393216 | tf_op jit(solution)/shard_map/all_to_all | solution.py:415
  152.7 0.2 unpack.1
  152.9 2.9 %collective-permute-start.2 = (f32[168,128]{1,0:T(8,128)S(1)}, f32[168,128]{1,0:T(8,128)S(1)}, u32[]{:S(2)}, u32[]{:S(2)}) collective-permute-start(f32[168,128]{1,0:T(8,128)S(1)} %get-tuple-element.11), channel_id=1, source_target_pairs={{0,4},{4,0},{1,5},{5,1},{2,6},{6,2},{3,7},{7,3},{8,12},{12,8},{9,1... | collective-permute-start | bytes 258056 | tf_op jit(solution)/shard_map/ppermute | solution.py:411
  155.8 0.9 collective-permute-done.2.back
  156.7 0.7 join.1
  (10 shorter events, 0.1 us)
Async XLA Ops:
  0.6 9.4 %collective-permute-start.1 = (f32[2,35,35]{2,0,1:T(2,128)}, f32[2,35,35]{2,0,1:T(2,128)S(1)}, u32[]{:S(2)}, u32[]{:S(2)}) collective-permute-start(f32[2,35,35]{2,0,1:T(2,128)} %param.12), channel_id=1, source_target_pairs={{0,4},{4,0},{1,5},{5,1},{2,6},{6,2},{3,7},{7,3},{8,12},{12,8},{9,1... | collective-permute-start | bytes 29408 | tf_op jit(solution)/shard_map/ppermute | solution.py:411
  3.9 0.7 copy-start.3
  4.6 0.9 copy-start
  6.2 3.8 %copy-start.5 = (f32[2,35,35]{2,0,1:T(2,128)S(1)}, f32[2,35,35]{2,0,1:T(2,128)}, u32[]{:S(2)}) copy-start(f32[2,35,35]{2,0,1:T(2,128)} %param.12) | copy-start | bytes 29404
  6.2 8.7 %collective-permute-start = (f32[168,128]{1,0:T(8,128)S(1)}, f32[168,128]{1,0:T(8,128)S(1)}, u32[]{:S(2)}, u32[]{:S(2)}) collective-permute-start(f32[168,128]{1,0:T(8,128)S(1)} %get-tuple-element.8), channel_id=1, source_target_pairs={{0,4},{4,0},{1,5},{5,1},{2,6},{6,2},{3,7},{7,3},{8,12},{12,8},{9,1... | collective-permute-start | bytes 258056 | tf_op jit(solution)/shard_map/ppermute | solution.py:411
  6.3 8.6 %all-to-all-start = ((f32[8,4,128]{2,1,0:T(4,128)}), f32[8,4,128]{2,1,0:T(4,128)S(1)}, u32[]{:S(2)}, u32[]{:S(2)}) async-start(f32[8,4,128]{2,1,0:T(4,128)} %get-tuple-element.9), calls=%async_computation | async-start | bytes 32768 | tf_op jit(solution)/shard_map/all_to_all | solution.py:434
  10.4 4.5 %copy-start.1 = (f32[4,35,256]{2,0,1:T(4,128)S(1)}, f32[4,35,256]{2,0,1:T(4,128)}, u32[]{:S(2)}) copy-start(f32[4,35,256]{2,0,1:T(4,128)} %param.10) | copy-start | bytes 430084
  10.5 0.6 copy-start.4
  11.1 0.7 slice-start
  16.3 10.7 %copy-start.10 = (f32[35]{0:T(128)S(1)}, f32[35]{0:T(128)}, u32[]{:S(2)}) copy-start(f32[35]{0:T(128)} %param.13) | copy-start | bytes 424
  16.3 10.8 %copy-start.6 = (f32[35]{0:T(128)S(1)}, f32[35]{0:T(128)}, u32[]{:S(2)}) copy-start(f32[35]{0:T(128)} %param.17) | copy-start | bytes 424
  16.3 10.8 %copy-start.7 = (f32[35]{0:T(128)S(1)}, f32[35]{0:T(128)}, u32[]{:S(2)}) copy-start(f32[35]{0:T(128)} %param.16) | copy-start | bytes 424
  16.3 10.8 %copy-start.8 = (f32[35]{0:T(128)S(1)}, f32[35]{0:T(128)}, u32[]{:S(2)}) copy-start(f32[35]{0:T(128)} %param.15) | copy-start | bytes 424
  16.3 10.8 %copy-start.9 = (f32[35]{0:T(128)S(1)}, f32[35]{0:T(128)}, u32[]{:S(2)}) copy-start(f32[35]{0:T(128)} %param.14) | copy-start | bytes 424
  16.3 24.9 %all-to-all-start.1 = ((f32[32,32,128]{2,1,0:T(8,128)}), f32[32,32,128]{2,1,0:T(8,128)S(1)}, u32[]{:S(2)}, u32[]{:S(2)}) async-start(f32[32,32,128]{2,1,0:T(8,128)} %pack.1), calls=%async_computation.1 | async-start | bytes 1048576 | tf_op jit(solution)/shard_map/all_to_all | solution.py:415
  27.0 14.2 %copy-start.2 = (f32[70,256]{1,0:T(8,128)S(1)}, f32[70,256]{1,0:T(8,128)}, u32[]{:S(2)}) copy-start(f32[70,256]{1,0:T(8,128)} %init_ref.1) | copy-start | bytes 215044
  152.9 3.9 %collective-permute-start.2 = (f32[168,128]{1,0:T(8,128)S(1)}, f32[168,128]{1,0:T(8,128)S(1)}, u32[]{:S(2)}, u32[]{:S(2)}) collective-permute-start(f32[168,128]{1,0:T(8,128)S(1)} %get-tuple-element.11), channel_id=1, source_target_pairs={{0,4},{4,0},{1,5},{5,1},{2,6},{6,2},{3,7},{7,3},{8,12},{12,8},{9,1... | collective-permute-start | bytes 258056 | tf_op jit(solution)/shard_map/ppermute | solution.py:411

commit v3 on v2

--- a/solution.py
+++ b/solution.py
@@ -87,15 +87,18 @@
     return pl.ds(pl.multiple_of(which * LANES, LANES), LANES)
 
 
-def split_kernel(core, torque, contact, send, counts):
+def count_kernel(core, contact, counts):
+    total = jnp.sum(contact[...].astype(f32), axis=1, keepdims=True)
+    for peer in range(8):
+        counts[peer] = jnp.broadcast_to(total, (4, LANES))
+
+
+def split_kernel(core, torque, contact, send):
     there = half_of(1 - core[0])
     send[...] = jnp.zeros_like(send)
     for t in range(4):
         send[t * PAD : t * PAD + DOF, :] = torque[:, t, there]
     send[4 * PAD : 4 * PAD + 4, :] = contact[:, there].astype(f32)
-    total = jnp.sum(contact[...].astype(f32), axis=1, keepdims=True)
-    for peer in range(8):
-        counts[peer] = jnp.broadcast_to(total, (4, LANES))
 
 
 def pack_kernel(core, torque, contact, back, totals, mass, tails, out, rows):
@@ -129,7 +132,7 @@
 
 
 def main_kernel(
-    chip, init_ref, recv, par, out, rows, fold, mb, ma, wide, cols, tau_b, stiff_b, damp_b, spring, fric, start, end, shift, diff, pos, vel, force, vec, corr
+    chip, init_ref, recv, par, out, rows, fold, mb, ma, wide, cols, tau_b, stiff_b, damp_b, spring, fric, start, end, shift, pos, vel, force, vec, corr
 ):
     for c in range(3):
         rows[c * LANES : (c + 1) * LANES, :] = jnp.concatenate(
@@ -152,12 +155,13 @@
             mb[k, i : i + 1, :] = fold[at : at + 1, :]
         mb[k, DOF:PAD, :] = jnp.zeros((PAD - DOF, LANES), f32)
 
-    def place_mass(k, carry):
-        for b, spread in enumerate(block_spread(mb[k])):
-            ma[b, k] = spread
+    def place_mass(n, carry):
+        for k in range(5):
+            for b, spread in enumerate(block_spread(mb[5 * n + k])):
+                ma[b, 5 * n + k] = spread
         return carry
 
-    lax.fori_loop(0, DOF, place_mass, 0)
+    lax.fori_loop(0, DOF // 5, place_mass, 0)
 
     mean = rows[ROW_COUNT : ROW_COUNT + 8, :] / ENV
     for t in range(STEPS):
@@ -177,93 +181,122 @@
 
     grav = gravity * (FINE * FINE * TURN)
 
-    def half_step(b, t, q, w, driven):
-        pull = spring[t] * q + fric[t] * w
-        if driven:
-            at = t * PAD if isinstance(t, int) else pl.multiple_of(t * PAD, 8)
-            pull = rows[pl.ds(at, PAD), :] * (FINE * DT * TURN) - pull
-        else:
-            pull = -pull
-        vec[0:PAD, :] = pull
+    def half_step(b, t, states, driven):
+        moved = []
+        for n, (q, w) in enumerate(states):
+            pull = spring[t] * q + fric[t] * w
+            if driven:
+                pull = rows[pl.ds(pl.multiple_of(t * PAD, 8), PAD), :] * (FINE * DT * TURN) - pull
+            else:
+                pull = -pull
+            vec[n, 0:PAD, :] = pull
+            moved.append(w)
         for k in range(DOF):
-            w = w + ma[b, k] * vec[k : k + 1, :]
-        return q + float(SUB) * w, w
-
-    def slice_step(b, q, w, driven):
-        q, w = half_step(b, 2 * b, q, w, driven)
-        return half_step(b, 2 * b + 1, q, w, driven)
-
-    def apply_wide(level, value):
-        vec[...] = value
-        total = None
+            mass = ma[b, k]
+            for n in range(len(states)):
+                moved[n] = moved[n] + mass * vec[n, k : k + 1, :]
+        return tuple((q + float(SUB) * w, w) for (q, _), w in zip(states, moved))
+
+    def slice_step(b, states, driven):
+        return half_step(b, 2 * b + 1, half_step(b, 2 * b, states, driven), driven)
+
+    def one_slice(b, q, w, driven):
+        return slice_step(b, ((q, w),), driven)[0]
+
+    def apply_wide(level, row_of):
+        low = high = None
         for k in range(2 * DOF):
-            term = wide[level, k] * vec[state_row(k) : state_row(k) + 1, :]
-            total = term if total is None else total + term
-        return total
+            row = row_of(state_row(k))
+            term = wide[level, k, :PAD, :] * row
+            low = term if low is None else low + term
+            if k < DOF:
+                term = wide[level, k, PAD:, :] * row
+                high = term if high is None else high + term
+        for k in range(DOF, 2 * DOF):
+            high = high + wide[level, k, PAD:, :] * row_of(state_row(k))
+        return low, high
 
     row80 = lax.broadcasted_iota(jnp.int32, (2 * PAD, LANES), 0)
     col_block = lane_index(2 * PAD) >> 5
 
-    def spread_columns(level, cg, value):
-        for c, spread in enumerate(block_spread(value)):
-            wide[level, 4 * cg + c] = spread
-
-    def first_columns(cg, carry):
-        col = 4 * cg + col_block
-        col = jnp.where(col < DOF, col, col + (PAD - DOF))
-        unit = jnp.where(row80 == col, 1.0, 0.0)
-
-        def one(b, qw):
-            return slice_step(b, qw[0], qw[1], False)
-
-        q, w = lax.fori_loop(0, GROUP, one, (unit[:PAD], unit[PAD:]))
-        value = jnp.concatenate([q, w], axis=0)
-        cols[cg] = value
-        spread_columns(0, cg, value)
+    def first_columns(pair, carry):
+        states = []
+        for n in range(2):
+            col = 4 * (2 * pair + n) + col_block
+            col = jnp.where(col < DOF, col, col + (PAD - DOF))
+            unit = jnp.where(row80 == col, 1.0, 0.0)
+            states.append((unit[:PAD], unit[PAD:]))
+        states = lax.fori_loop(0, GROUP, lambda b, now: slice_step(b, now, False), tuple(states))
+        for n in range(2):
+            cols[2 * pair + n, :PAD, :] = states[n][0]
+            cols[2 * pair + n, PAD:, :] = states[n][1]
         return carry
 
-    lax.fori_loop(0, 18, first_columns, 0)
-    for level, by in ((1, 1), (2, 2)):
-
-        def more_columns(cg, carry, level=level, by=by):
-            value = apply_wide(level - 1, shifted(cols[cg], by))
-            cols[cg] = value
-            spread_columns(level, cg, value)
+    lax.fori_loop(0, 9, first_columns, 0)
+
+    def spread_columns(level, by):
+        def some(n, carry):
+            for m in range(3):
+                value = cols[3 * n + m]
+                for c, spread in enumerate(block_spread(value)):
+                    wide[level, 4 * (3 * n + m) + c] = spread
+                if by:
+                    cols[3 * n + m] = shifted(value, by)
             return carry
 
-        lax.fori_loop(0, 18, more_columns, 0)
-
-    def scan_groups(value):
-        value = value + apply_wide(0, shifted(value, 1))
-        value = value + apply_wide(1, shifted(value, 2))
-        diff[0] = value
-
-        def more(i, running):
-            return diff[0] + apply_wide(2, shifted(running, 4))
-
-        return lax.fori_loop(0, 7, more, value)
+        lax.fori_loop(0, 6, some, 0)
+
+    def more_columns(level):
+        def one(cg, carry):
+            low, high = apply_wide(level - 1, lambda r: cols[cg, r : r + 1, :])
+            cols[cg, :PAD, :] = low
+            cols[cg, PAD:, :] = high
+            return carry
+
+        lax.fori_loop(0, 18, one, 0)
+
+    spread_columns(0, 1)
+    more_columns(1)
+    spread_columns(1, 2)
+    more_columns(2)
+    spread_columns(2, 0)
+
+    def scan_groups(q, w):
+        def add_earlier(level, by, slot, base, state):
+            vec[slot, :PAD, :] = shifted(state[0], by)
+            vec[slot, PAD:, :] = shifted(state[1], by)
+            low, high = apply_wide(level, lambda r: vec[slot, r : r + 1, :])
+            return base[0] + low, base[1] + high
+
+        state = (q, w)
+        state = add_earlier(0, 1, 0, state, state)
+        state = base = add_earlier(1, 2, 1, state, state)
+        for n in range(7):
+            state = add_earlier(2, 4, n % 2, base, state)
+        return state
 
     first = (lane_index(2 * PAD) & 31) == 0
     back_by = LANES - chip[0]
-    vec[...] = jnp.zeros_like(vec)
-    vec[0:DOF, :] = init_ref[:DOF, half_of(chip[1])] * TURN
-    vec[PAD : PAD + DOF, :] = init_ref[DOF:, half_of(chip[1])] * (FINE * TURN)
-    init = jnp.where(first, pltpu.roll(vec[...], back_by, 1), 0.0)
+    vec[0] = jnp.zeros((2 * PAD, LANES), f32)
+    vec[0, 0:DOF, :] = init_ref[:DOF, half_of(chip[1])] * TURN
+    vec[0, PAD : PAD + DOF, :] = init_ref[DOF:, half_of(chip[1])] * (FINE * TURN)
+    init = jnp.where(first, pltpu.roll(vec[0], back_by, 1), 0.0)
 
     def driven_slice(b, qw):
-        return slice_step(b, qw[0], qw[1], True)
+        return one_slice(b, qw[0], qw[1], True)
 
     q, w = lax.fori_loop(0, GROUP, driven_slice, (init[:PAD], init[PAD:]))
-    ends = scan_groups(jnp.concatenate([q, w], axis=0))
-    entry = jnp.where(first, init, shifted(ends, 1))
+    q, w = scan_groups(q, w)
+    first = first[:PAD]
+    entry = jnp.where(first, init[:PAD], shifted(q, 1)), jnp.where(first, init[PAD:], shifted(w, 1))
 
     def driven_keep(b, qw):
-        start[b] = jnp.concatenate(qw, axis=0)
-        qw = slice_step(b, qw[0], qw[1], True)
-        end[b] = jnp.concatenate(qw, axis=0)
+        start[b, :PAD, :], start[b, PAD:, :] = qw
+        qw = one_slice(b, qw[0], qw[1], True)
+        end[b, :PAD, :], end[b, PAD:, :] = qw
         return qw
 
-    lax.fori_loop(0, GROUP, driven_keep, (entry[:PAD], entry[PAD:]))
+    lax.fori_loop(0, GROUP, driven_keep, entry)
 
     corr[...] = jnp.zeros_like(corr)
 
@@ -299,24 +332,26 @@
                 shift[b, half : half + PAD, :] = part - end[b, half : half + PAD, :]
 
         def chain(b, qw):
-            q, w = slice_step(b, qw[0], qw[1], False)
+            q, w = one_slice(b, qw[0], qw[1], False)
             return q + shift[b, :PAD, :], w + shift[b, PAD:, :]
 
         q, w = lax.fori_loop(1, GROUP, chain, (shift[0, :PAD, :], shift[0, PAD:, :]))
-        entry = shifted(scan_groups(jnp.concatenate([q, w], axis=0)), 1)
+        q, w = scan_groups(q, w)
 
         def keep(b, state):
             q, w, largest = state
-            start[b] = start[b] + jnp.concatenate([q, w], axis=0)
+            start[b, :PAD, :] = start[b, :PAD, :] + q
+            start[b, PAD:, :] = start[b, PAD:, :] + w
             q, w = chain(b, (q, w))
-            end[b] = end[b] + jnp.concatenate([q, w], axis=0)
+            end[b, :PAD, :] = end[b, :PAD, :] + q
+            end[b, PAD:, :] = end[b, PAD:, :] + w
             dq = q * (1.0 / TURN)
             dv = w * (1.0 / (TURN * FINE))
             square = jnp.sum(dq * dq + dv * dv, axis=0, keepdims=True)
             return q, w, jnp.maximum(largest, square)
 
         _, _, largest = lax.fori_loop(
-            0, GROUP, keep, (entry[:PAD], entry[PAD:], jnp.zeros((1, LANES), f32))
+            0, GROUP, keep, (shifted(q, 1), shifted(w, 1), jnp.zeros((1, LANES), f32))
         )
         group = lane_index(1) & 31
         for by in (16, 8, 4, 2, 1):
@@ -392,11 +427,10 @@
         (GROUP, 2 * PAD, LANES),
         (GROUP, 2 * PAD, LANES),
         (GROUP, 2 * PAD, LANES),
-        (1, 2 * PAD, LANES),
         (BLOCKS, *tile),
         (BLOCKS, *tile),
         (BLOCKS, *tile),
-        (2 * PAD, LANES),
+        (2, 2 * PAD, LANES),
         (8, LANES),
     ]
     return local_call(main_kernel, "parareal", [(CHIPS, 3, 4, LANES)], scratch, chip, init, recv, par)
@@ -429,7 +463,8 @@
 
     mass_back = swapped(mass_inverse)
     torque = torque.transpose(1, 0, 2)
-    send, counts = local_call(split_kernel, "split", [SWAP, (8, 4, LANES)], [], core[None], torque, contact)
+    counts = local_call(count_kernel, "count", [(8, 4, LANES)], [], core[None], contact)
+    send = local_call(split_kernel, "split", [SWAP], [], core[None], torque, contact)
     back = swapped(send)
     counts = lax.all_to_all(counts, ("c", "y"), split_axis=0, concat_axis=0, tiled=True)
     totals = counts.reshape(2, BLOCKS, 4, LANES).sum(axis=1).reshape(8, LANES)
@@ -457,7 +492,10 @@
         mass_rows,
         mass_tails,
     )
-    solved = main_call(jnp.stack([chip, core]), init_state, exchanged(sent), param_table(*vectors))
+    sent, place, par, init = lax.optimization_barrier(
+        (sent, jnp.stack([chip, core]), param_table(*vectors), init_state)
+    )
+    solved = main_call(place, init, exchanged(sent), par)
     mine, send = local_call(
         unpack_kernel, "unpack", [SWAP, SWAP], [(3 * LANES, LANES)], core[None], exchanged(solved)
     )

time: 158 us -> 149 us (0.943)
  blocking collectives: 17.3 us -> 41.9 us
  waiting for transfers between devices: 17.9 us -> 1.55 us
  starting transfers between devices: 20.7 us -> 9.99 us
  Pallas kernels: 97.2 us -> 90.3 us
    all_to_all x1 -> x2, blocking collectives: 17.3 us -> 41.9 us  [exchanged(): return lax.all_to_all(value, PEERS, split_axis=0, concat_axis=0, tiled=True)]
    all_to_all x1 -> x0, waiting for transfers between devices: 13.9 us -> none  [exchanged(): return lax.all_to_all(value, PEERS, split_axis=0, concat_axis=0, tiled=True)]
    all_to_all x1 -> x0, starting transfers between devices: 10.7 us -> none  [exchanged(): return lax.all_to_all(value, PEERS, split_axis=0, concat_axis=0, tiled=True)]
    pallas_call x5 -> x6, Pallas kernels: 97.2 us -> 90.3 us  [local_call(): pl.pallas_call(kernel, in_specs=[smem] + [vmem] * len(arrays), out_specs=...]
    all_to_all x1, starting transfers between devices: 3.75 us -> 6.46 us  [shards(): lax.all_to_all(counts, ('c', 'y'), split_axis=0, concat_axis=0, tiled=True)]
    ppermute x3, starting transfers between devices: 6.24 us -> 3.53 us  [swapped(): return lax.ppermute(value, 'c', [(0, 1), (1, 0)])]
    all_to_all x1, waiting for transfers between devices: 3.05 us -> 0.62 us  [shards(): lax.all_to_all(counts, ('c', 'y'), split_axis=0, concat_axis=0, tiled=True)]
    unnamed x23 -> x21, local copies, waits for them, and re-layouts: 2.29 us -> 3.62 us
  transfers between devices with their start and end apart: 5 -> 4, of which waited for: 3 -> 2; matrix products, arithmetic and copies ran while one was open for 0% -> 0% of each run, Pallas kernels for 0% -> 0%
where the time goes in v3:
time: 149 us
  Pallas kernels  90.3 us (61%)
  blocking collectives  41.9 us (28%)
  starting transfers between devices  9.99 us (7%)
  local copies, waits for them, and re-layouts  4 us (3%)
  waiting for transfers between devices  1.55 us (1%)
    pallas_call x6, Pallas kernels, local_call(): pl.pallas_call(kernel, in_specs=[smem] + [vmem] * len(arrays), out_specs=...  90.3 us
    all_to_all x2, blocking collectives, exchanged(): return lax.all_to_all(value, PEERS, split_axis=0, concat_axis=0, tiled=True)  41.9 us
    all_to_all x1, starting transfers between devices, shards(): lax.all_to_all(counts, ('c', 'y'), split_axis=0, concat_axis=0, tiled=True)  6.46 us
    unnamed x21, local copies, waits for them, and re-layouts  3.62 us
    ppermute x3, starting transfers between devices, swapped(): return lax.ppermute(value, 'c', [(0, 1), (1, 0)])  3.53 us
  transfers between devices with their start and end apart: 4, of which 2 were waited for; matrix products, arithmetic and copies ran while one was open for 0% of the time, Pallas kernels for 0%

profile of v3, /device:TPU:1, one launch (start us, length us, event | category | flops | bytes accessed | tf_op | source)
XLA Modules:
  0.0 148.8 jit_solution(7361355286568199524)
XLA Ops:
  0.6 0.0 copy-start.3
  0.6 0.0 copy-start.4
  0.7 0.7 copy-done.3
  1.3 0.7 count.1
  2.0 6.5 %all-to-all-start = ((f32[8,4,128]{2,1,0:T(4,128)}), f32[8,4,128]{2,1,0:T(4,128)S(1)}, u32[]{:S(2)}, u32[]{:S(2)}) async-start(f32[8,4,128]{2,1,0:T(4,128)} %count.1), calls=%async_computation | async-start | bytes 32768 | tf_op jit(solution)/shard_map/all_to_all | solution.py:469
  8.5 0.0 copy-done.4
  8.5 0.2 collective-permute-start.1
  8.7 0.0 copy-start
  8.7 0.9 copy-done
  9.6 0.1 split.1
  9.6 0.4 collective-permute-start
  10.0 0.0 copy-start.5
  10.0 0.0 copy-start.6
  10.0 0.1 pad_add_fusion.chip
  10.1 0.6 copy-done.5
  10.7 0.0 copy-done.6
  10.7 0.0 copy-start.7
  10.7 0.0 copy-start.8
  10.7 0.6 copy-done.7
  11.4 0.0 copy-done.8
  11.4 0.0 copy-start.9
  11.4 0.6 copy-done.9
  12.1 0.1 copy.26
  12.2 0.0 collective-permute-done.1
  12.2 0.1 maximum_select_fusion
  12.3 0.1 rev.3
  12.4 0.1 fusion
  12.5 0.0 copy-start.1
  12.5 0.1 reshape.18
  12.7 0.1 copy.27
  12.7 0.6 all-to-all-done
  13.4 0.0 collective-permute-done.back
  13.4 0.0 copy-done.1
  13.4 0.5 pack.1
  13.9 0.0 copy-start.2
  13.9 24.7 %all_to_all.15.recv = f32[32,32,128]{2,1,0:T(8,128)S(1)} all-to-all(f32[32,32,128]{2,1,0:T(8,128)S(1)} %pack.1), channel_id=1, replica_groups=mesh['x'=4,'z'=8,'c'=2,'y'=4] {'x','z'}, dimensions={0} | all-to-all | bytes 1048576 | tf_op jit(solution)/shard_map/all_to_all | solution.py:449
  38.6 0.0 copy-done.2
  38.6 88.1 %parareal.1 = f32[32,3,4,128]{3,2,1,0:T(4,128)S(1)} custom-call(s32[2]{0:T(128)S(1)} %pad_add_fusion.chip, f32[70,256]{1,0:T(8,128)S(1)} %copy-done.2, f32[32,32,128]{2,1,0:T(8,128)S(1)} %all_to_all.15.recv, f32[40,8]{1,0:T(8,128)S(1)} %pad.35.par), custom_call_target="tpu_custom_call" | custom-call | tf_op jit(solution)/shard_map/parareal/pallas_call | solution.py:402
  126.7 17.3 %all_to_all.16.recv = f32[32,3,4,128]{3,2,1,0:T(4,128)S(1)} all-to-all(f32[32,3,4,128]{3,2,1,0:T(4,128)S(1)} %parareal.1), channel_id=1, replica_groups=mesh['x'=4,'z'=8,'c'=2,'y'=4] {'x','z'}, dimensions={0} | all-to-all | bytes 393216 | tf_op jit(solution)/shard_map/all_to_all | solution.py:449
  144.0 0.2 unpack.1
  144.2 2.9 %collective-permute-start.2 = (f32[168,128]{1,0:T(8,128)S(1)}, f32[168,128]{1,0:T(8,128)S(1)}, u32[]{:S(2)}, u32[]{:S(2)}) collective-permute-start(f32[168,128]{1,0:T(8,128)S(1)} %get-tuple-element.15), channel_id=1, source_target_pairs={{0,4},{4,0},{1,5},{5,1},{2,6},{6,2},{3,7},{7,3},{8,12},{12,8},{9,1... | collective-permute-start | bytes 258056 | tf_op jit(solution)/shard_map/ppermute | solution.py:445
  147.1 0.9 collective-permute-done.2.back
  148.0 0.7 join.1
  (11 shorter events, 0.1 us)
Async XLA Ops:
  0.6 0.7 copy-start.3
  0.6 7.8 %copy-start.4 = (f32[2,35,35]{2,0,1:T(2,128)S(1)}, f32[2,35,35]{2,0,1:T(2,128)}, u32[]{:S(2)}) copy-start(f32[2,35,35]{2,0,1:T(2,128)} %param.12) | copy-start | bytes 29404
  2.0 11.3 %all-to-all-start = ((f32[8,4,128]{2,1,0:T(4,128)}), f32[8,4,128]{2,1,0:T(4,128)S(1)}, u32[]{:S(2)}, u32[]{:S(2)}) async-start(f32[8,4,128]{2,1,0:T(4,128)} %count.1), calls=%async_computation | async-start | bytes 32768 | tf_op jit(solution)/shard_map/all_to_all | solution.py:469
  8.5 3.7 %collective-permute-start.1 = (f32[2,35,35]{2,0,1:T(2,128)S(1)}, f32[2,35,35]{2,0,1:T(2,128)S(1)}, u32[]{:S(2)}, u32[]{:S(2)}) collective-permute-start(f32[2,35,35]{2,0,1:T(2,128)S(1)} %copy-done.4), channel_id=1, source_target_pairs={{0,4},{4,0},{1,5},{5,1},{2,6},{6,2},{3,7},{7,3},{8,12},{12,8},{9,1... | collective-permute-start | bytes 29408 | tf_op jit(solution)/shard_map/ppermute | solution.py:445
  8.7 0.9 copy-start
  9.6 3.8 %collective-permute-start = (f32[168,128]{1,0:T(8,128)S(1)}, f32[168,128]{1,0:T(8,128)S(1)}, u32[]{:S(2)}, u32[]{:S(2)}) collective-permute-start(f32[168,128]{1,0:T(8,128)S(1)} %split.1), channel_id=1, source_target_pairs={{0,4},{4,0},{1,5},{5,1},{2,6},{6,2},{3,7},{7,3},{8,12},{12,8},{9,1... | collective-permute-start | bytes 258056 | tf_op jit(solution)/shard_map/ppermute | solution.py:445
  10.0 0.7 copy-start.5
  10.0 0.7 copy-start.6
  10.7 0.7 copy-start.7
  10.7 0.7 copy-start.8
  11.4 0.7 copy-start.9
  12.5 0.9 copy-start.1
  13.9 24.7 %copy-start.2 = (f32[70,256]{1,0:T(8,128)S(1)}, f32[70,256]{1,0:T(8,128)}, u32[]{:S(2)}) copy-start(f32[70,256]{1,0:T(8,128)} %init_ref) | copy-start | bytes 215044
  144.2 3.9 %collective-permute-start.2 = (f32[168,128]{1,0:T(8,128)S(1)}, f32[168,128]{1,0:T(8,128)S(1)}, u32[]{:S(2)}, u32[]{:S(2)}) collective-permute-start(f32[168,128]{1,0:T(8,128)S(1)} %get-tuple-element.15), channel_id=1, source_target_pairs={{0,4},{4,0},{1,5},{5,1},{2,6},{6,2},{3,7},{7,3},{8,12},{12,8},{9,1... | collective-permute-start | bytes 258056 | tf_op jit(solution)/shard_map/ppermute | solution.py:445

commit v4 on v3

--- a/solution.py
+++ b/solution.py
@@ -26,7 +26,7 @@
 DT = 0.05
 FINE = DT / SUB
 TURN = 1.0 / (2.0 * math.pi)
-SINE = (6.283182595389212, -16.20867027746649, 16.7609745050196, -9.530799181282873, 3.0583252710952205)
+SINE = tuple(4.0 * c for c in (6.283182595389212, -16.20867027746649, 16.7609745050196, -9.530799181282873, 3.0583252710952205))
 
 ROW_CONTACT = STEPS * PAD
 ROW_COUNT = ROW_CONTACT + 8
@@ -38,6 +38,7 @@
 MASS_ROWS = 5
 CHUNKS = IN_ROWS + GROUP * MASS_ROWS
 VMEM_LIMIT = 24 * 1024 * 1024
+ALL_VMEM = 67_043_328
 
 f32 = jnp.float32
 
@@ -87,29 +88,44 @@
     return pl.ds(pl.multiple_of(which * LANES, LANES), LANES)
 
 
-def count_kernel(core, contact, counts):
-    total = jnp.sum(contact[...].astype(f32), axis=1, keepdims=True)
+def split_kernel(
+    core, contact, torque, mass, v0, v1, v2, v3, v4,
+    counts, table, mass_out, own, send,
+    contact_in, torque_in, vectors_in, spare, sems,
+):
+    vectors = (v0, v1, v2, v3, v4)
+    pairs = [(contact, contact_in), (torque, torque_in), (mass, mass_out)]
+    pairs += [(v, vectors_in.at[i]) for i, v in enumerate(vectors)]
+    copies = [pltpu.make_async_copy(a, b, sems.at[i]) for i, (a, b) in enumerate(pairs)]
+    for copy in copies:
+        copy.start()
+    own[...] = jnp.zeros_like(own)
+    send[...] = jnp.zeros_like(send)
+    spare[...] = jnp.zeros_like(spare)
+    copies[0].wait()
+    total = jnp.sum(contact_in[...].astype(f32), axis=1, keepdims=True)
     for peer in range(8):
         counts[peer] = jnp.broadcast_to(total, (4, LANES))
-
-
-def split_kernel(core, torque, contact, send):
-    there = half_of(1 - core[0])
-    send[...] = jnp.zeros_like(send)
-    for t in range(4):
-        send[t * PAD : t * PAD + DOF, :] = torque[:, t, there]
-    send[4 * PAD : 4 * PAD + 4, :] = contact[:, there].astype(f32)
-
-
-def pack_kernel(core, torque, contact, back, totals, mass, tails, out, rows):
+    for copy in copies[3:]:
+        copy.wait()
+    for i in range(len(vectors)):
+        spare[i : i + 1, 0:DOF] = vectors_in[i]
+    table[...] = spare[...].T[0:PAD, 0:8]
+    copies[2].wait()
+    copies[1].wait()
+    for ref, which in ((own, core[0]), (send, 1 - core[0])):
+        part = half_of(which)
+        for t in range(4):
+            ref[t * PAD : t * PAD + DOF, :] = torque_in[:, t, part]
+        ref[4 * PAD : 4 * PAD + 4, :] = contact_in[:, part].astype(f32)
+
+
+def pack_kernel(core, own, back, totals, mass, tails, out, rows):
     me = core[0]
-    here = half_of(me)
     rows[...] = jnp.zeros_like(rows)
-    for t in range(4):
-        rows[pl.ds(pl.multiple_of((4 * me + t) * PAD, 8), DOF), :] = torque[:, t, here]
-        rows[pl.ds(pl.multiple_of((4 * (1 - me) + t) * PAD, 8), PAD), :] = back[t * PAD : (t + 1) * PAD, :]
-    own = contact[:, here].astype(f32)
-    other = back[4 * PAD : 4 * PAD + 4, :]
+    for ref, which in ((own, me), (back, 1 - me)):
+        rows[pl.ds(pl.multiple_of(which * 4 * PAD, 8), 4 * PAD), :] = ref[0 : 4 * PAD, :]
+    own, other = (ref[4 * PAD : 4 * PAD + 4, :] for ref in (own, back))
     rows[ROW_CONTACT : ROW_CONTACT + 8, :] = jnp.where(
         me == 0, jnp.concatenate([own, other]), jnp.concatenate([other, own])
     )
@@ -219,14 +235,23 @@
     row80 = lax.broadcasted_iota(jnp.int32, (2 * PAD, LANES), 0)
     col_block = lane_index(2 * PAD) >> 5
 
+    def first_half(base, q, w):
+        for c in range(4):
+            k = base + c
+            r = jnp.minimum(jnp.where(k < DOF, k, k - DOF), DOF - 1)
+            row = jnp.where(k < DOF, spring[0, pl.ds(r, 1), :], fric[0, pl.ds(r, 1), :])
+            w = w - jnp.where(col_block[:PAD] == c, ma[0, r] * row, 0.0)
+        return q + float(SUB) * w, w
+
     def first_columns(pair, carry):
         states = []
         for n in range(2):
             col = 4 * (2 * pair + n) + col_block
             col = jnp.where(col < DOF, col, col + (PAD - DOF))
             unit = jnp.where(row80 == col, 1.0, 0.0)
-            states.append((unit[:PAD], unit[PAD:]))
-        states = lax.fori_loop(0, GROUP, lambda b, now: slice_step(b, now, False), tuple(states))
+            states.append(first_half(4 * (2 * pair + n), unit[:PAD], unit[PAD:]))
+        states = half_step(0, 1, states, False)
+        states = lax.fori_loop(1, GROUP, lambda b, now: slice_step(b, now, False), states)
         for n in range(2):
             cols[2 * pair + n, :PAD, :] = states[n][0]
             cols[2 * pair + n, PAD:, :] = states[n][1]
@@ -314,7 +339,7 @@
                 poly = SINE[4] * s + SINE[3]
                 for coef in (SINE[2], SINE[1], SINE[0]):
                     poly = poly * s + coef
-                sine = (f * (1.0 - 4.0 * s)) * poly
+                sine = (f * (0.25 - s)) * poly
                 force[e] = tau_b[j, e] - stiff_b[j, e] * p - damp_b[j, e] * vel[e] - grav * sine
             acc = [vel[e] for e in range(BLOCKS)]
             for k in range(DOF):
@@ -436,11 +461,6 @@
     return local_call(main_kernel, "parareal", [(CHIPS, 3, 4, LANES)], scratch, chip, init, recv, par)
 
 
-def param_table(*vectors):
-    table = jnp.stack([jnp.pad(v, (0, PAD - DOF)) for v in vectors], axis=1)
-    return jnp.pad(table, ((0, 0), (0, 8 - len(vectors))))
-
-
 def swapped(value):
     return lax.ppermute(value, "c", [(0, 1), (1, 0)])
 
@@ -461,20 +481,43 @@
     core = lax.axis_index("c").astype(jnp.int32)
     chip = (lax.axis_index("x") * lax.axis_size("z") + lax.axis_index("z")).astype(jnp.int32)
 
-    mass_back = swapped(mass_inverse)
-    torque = torque.transpose(1, 0, 2)
-    counts = local_call(count_kernel, "count", [(8, 4, LANES)], [], core[None], contact)
-    send = local_call(split_kernel, "split", [SWAP], [], core[None], torque, contact)
+    smem = pl.BlockSpec(memory_space=pltpu.SMEM)
+    hbm = pl.BlockSpec(memory_space=pltpu.HBM)
+    vmem = pl.BlockSpec(memory_space=pltpu.VMEM)
+    steps, dof = torque.shape[:2]
+    shapes = [(8, 4, LANES), (PAD, 8), (dof, 2, dof), SWAP, SWAP]
+    counts, par, mass, own, send = pl.pallas_call(
+        split_kernel,
+        in_specs=[smem] + [hbm] * 8,
+        out_specs=(vmem,) * len(shapes),
+        out_shape=tuple(jax.ShapeDtypeStruct(shape, f32) for shape in shapes),
+        scratch_shapes=[
+            pltpu.VMEM((steps, 2 * LANES), jnp.int32),
+            pltpu.VMEM((dof, steps, 2 * LANES), f32),
+            pltpu.VMEM((5, 1, dof), f32),
+            pltpu.VMEM((LANES, LANES), f32),
+            pltpu.SemaphoreType.DMA((8,)),
+        ],
+        compiler_params=pltpu.CompilerParams(vmem_limit_bytes=ALL_VMEM),
+        name="split",
+    )(
+        core[None],
+        contact,
+        torque.transpose(1, 0, 2),
+        mass_inverse.transpose(1, 0, 2),
+        *[v[None] for v in vectors],
+    )
     back = swapped(send)
     counts = lax.all_to_all(counts, ("c", "y"), split_axis=0, concat_axis=0, tiled=True)
     totals = counts.reshape(2, BLOCKS, 4, LANES).sum(axis=1).reshape(8, LANES)
     order = core == 0
+    mass_back = swapped(mass)
     matrices = folded(
         jnp.where(
             order,
-            jnp.concatenate([mass_inverse, mass_back]),
-            jnp.concatenate([mass_back, mass_inverse]),
-        )
+            jnp.concatenate([mass, mass_back], axis=1),
+            jnp.concatenate([mass_back, mass], axis=1),
+        ).transpose(1, 0, 2)
     )
     mass_rows = matrices[:, : MASS_ROWS * LANES].reshape(GROUP * MASS_ROWS, LANES)
     mass_tails = matrices[:, MASS_ROWS * LANES :].T
@@ -485,15 +528,14 @@
         [(CHIPS, CHUNKS, LANES)],
         [(3 * LANES, LANES)],
         core[None],
-        torque,
-        contact,
+        own,
         back,
         totals,
         mass_rows,
         mass_tails,
     )
     sent, place, par, init = lax.optimization_barrier(
-        (sent, jnp.stack([chip, core]), param_table(*vectors), init_state)
+        (sent, jnp.stack([chip, core]), par, init_state)
     )
     solved = main_call(place, init, exchanged(sent), par)
     mine, send = local_call(

time: 149 us -> 148 us (level)
  local copies, waits for them, and re-layouts: 4 us -> 0.35 us
  waiting for transfers between devices: 1.55 us -> 4.67 us
    unnamed x21 -> x9, local copies, waits for them, and re-layouts: 3.62 us -> 0.1 us
    pallas_call x6 -> x4, Pallas kernels: 90.3 us -> 87.7 us  [local_call(): pl.pallas_call(kernel, in_specs=[smem] + [vmem] * len(arrays), out_specs=...]
    all_to_all x1, waiting for transfers between devices: 0.62 us -> 3.12 us  [shards(): lax.all_to_all(counts, ('c', 'y'), split_axis=0, concat_axis=0, tiled=True)]
    pallas_call x0 -> x1, Pallas kernels: none -> 1.75 us  [shards(): pl.pallas_call(split_kernel, in_specs=[smem] + [hbm] * 8, out_specs=(vmem...]
  transfers between devices with their start and end apart: 4 -> 4, of which waited for: 2 -> 3; matrix products, arithmetic and copies ran while one was open for 0% -> 0% of each run, Pallas kernels for 0% -> 0%
where the time goes in v4:
time: 148 us; the launch traced here: 147 us
  Pallas kernels  89.5 us (60%)
  blocking collectives  42 us (28%)
  starting transfers between devices  9.91 us (7%)
  waiting for transfers between devices  4.67 us (3%)
    pallas_call x4, Pallas kernels, local_call(): pl.pallas_call(kernel, in_specs=[smem] + [vmem] * len(arrays), out_specs=...  87.7 us
    all_to_all x2, blocking collectives, exchanged(): return lax.all_to_all(value, PEERS, split_axis=0, concat_axis=0, tiled=True)  42 us
    all_to_all x1, starting transfers between devices, shards(): lax.all_to_all(counts, ('c', 'y'), split_axis=0, concat_axis=0, tiled=True)  6.47 us
    ppermute x3, starting transfers between devices, swapped(): return lax.ppermute(value, 'c', [(0, 1), (1, 0)])  3.44 us
    all_to_all x1, waiting for transfers between devices, shards(): lax.all_to_all(counts, ('c', 'y'), split_axis=0, concat_axis=0, tiled=True)  3.12 us
  transfers between devices with their start and end apart: 4, of which 3 were waited for; matrix products, arithmetic and copies ran while one was open for 0% of the time, Pallas kernels for 0%

profile of v4, /device:TPU:1, one launch (start us, length us, event | category | flops | bytes accessed | tf_op | source)
XLA Modules:
  0.0 147.4 jit_solution(9723947983893204409)
XLA Ops:
  0.6 1.7 %split.1 = (f32[8,4,128]{2,1,0:T(4,128)}, f32[40,8]{1,0:T(8,128)}, f32[35,2,35]{2,1,0:T(2,128)}, f32[168,128]{1,0:T(8,128)}, f32[168,128]{1,0:T(8,128)}) custom-call(s32[1]{0:T(128)} %bitcast.core, s32[4,256]{1,0:T(4,128)} %contact.1, f32[35,4,256]{2,1,0:T(4,128)} %bitcast.18, f32[35,2,35]{2,1,0:T(2,128)} %bitcast.19, f32[1,35]{1,0:T(1,128)} %bitcast.20, ...), custom_call_target="tpu_custom_call" | custom-call | tf_op jit(solution)/shard_map/split/pallas_call | solution.py:489
  2.4 0.0 copy-start.3
  2.4 6.5 %all-to-all-start = ((f32[8,4,128]{2,1,0:T(4,128)}), f32[8,4,128]{2,1,0:T(4,128)S(1)}, u32[]{:S(2)}, u32[]{:S(2)}) async-start(f32[8,4,128]{2,1,0:T(4,128)} %get-tuple-element.17), calls=%async_computation | async-start | bytes 32768 | tf_op jit(solution)/shard_map/all_to_all | solution.py:511
  8.9 0.0 copy-done.3
  8.9 0.2 collective-permute-start.1
  9.1 0.3 collective-permute-start
  9.4 0.1 pad_add_fusion.chip
  9.5 0.6 collective-permute-done.1
  10.1 0.1 fusion
  10.2 0.1 rev.3
  10.3 0.1 fusion.1
  10.4 0.0 copy-start
  10.4 0.1 reshape.18
  10.6 0.1 copy.14
  10.6 3.1 %all-to-all-done = f32[8,4,128]{2,1,0:T(4,128)S(1)} async-done(((f32[8,4,128]{2,1,0:T(4,128)}), f32[8,4,128]{2,1,0:T(4,128)S(1)}, u32[]{:S(2)}, u32[]{:S(2)}) %all-to-all-start) | async-done | bytes 16416 | tf_op jit(solution)/shard_map/all_to_all | solution.py:511
  13.8 0.0 collective-permute-done.back
  13.8 0.0 copy-done
  13.8 0.5 pack.1
  14.3 0.0 copy-start.1
  14.3 0.0 copy-start.2
  14.3 24.7 %all_to_all.15.recv = f32[32,32,128]{2,1,0:T(8,128)S(1)} all-to-all(f32[32,32,128]{2,1,0:T(8,128)S(1)} %pack.1), channel_id=1, replica_groups=mesh['x'=4,'z'=8,'c'=2,'y'=4] {'x','z'}, dimensions={0} | all-to-all | bytes 1048576 | tf_op jit(solution)/shard_map/all_to_all | solution.py:469
  39.0 0.0 copy-done.1
  39.0 0.0 copy-done.2
  39.0 86.3 %parareal.1 = f32[32,3,4,128]{3,2,1,0:T(4,128)S(1)} custom-call(s32[2]{0:T(128)S(1)} %pad_add_fusion.chip, f32[70,256]{1,0:T(8,128)S(1)} %copy-done.1, f32[32,32,128]{2,1,0:T(8,128)S(1)} %all_to_all.15.recv, f32[40,8]{1,0:T(8,128)S(1)} %copy-done.2), custom_call_target="tpu_custom_call" | custom-call | tf_op jit(solution)/shard_map/parareal/pallas_call | solution.py:427
  125.3 17.3 %all_to_all.16.recv = f32[32,3,4,128]{3,2,1,0:T(4,128)S(1)} all-to-all(f32[32,3,4,128]{3,2,1,0:T(4,128)S(1)} %parareal.1), channel_id=1, replica_groups=mesh['x'=4,'z'=8,'c'=2,'y'=4] {'x','z'}, dimensions={0} | all-to-all | bytes 393216 | tf_op jit(solution)/shard_map/all_to_all | solution.py:469
  142.6 0.2 unpack.1
  142.8 2.9 %collective-permute-start.2 = (f32[168,128]{1,0:T(8,128)S(1)}, f32[168,128]{1,0:T(8,128)S(1)}, u32[]{:S(2)}, u32[]{:S(2)}) collective-permute-start(f32[168,128]{1,0:T(8,128)S(1)} %get-tuple-element.25), channel_id=1, source_target_pairs={{0,4},{4,0},{1,5},{5,1},{2,6},{6,2},{3,7},{7,3},{8,12},{12,8},{9,1... | collective-permute-start | bytes 258056 | tf_op jit(solution)/shard_map/ppermute | solution.py:465
  145.7 0.9 collective-permute-done.2.back
  146.6 0.7 join.1
  (6 shorter events, 0.0 us)
Async XLA Ops:
  2.4 6.5 %copy-start.3 = (f32[35,2,35]{2,1,0:T(2,128)S(1)}, f32[35,2,35]{2,1,0:T(2,128)}, u32[]{:S(2)}) copy-start(f32[35,2,35]{2,1,0:T(2,128)} %get-tuple-element.18) | copy-start | bytes 29404
  2.4 11.4 %all-to-all-start = ((f32[8,4,128]{2,1,0:T(4,128)}), f32[8,4,128]{2,1,0:T(4,128)S(1)}, u32[]{:S(2)}, u32[]{:S(2)}) async-start(f32[8,4,128]{2,1,0:T(4,128)} %get-tuple-element.17), calls=%async_computation | async-start | bytes 32768 | tf_op jit(solution)/shard_map/all_to_all | solution.py:511
  8.9 1.2 collective-permute-start.1
  9.1 4.7 %collective-permute-start = (f32[168,128]{1,0:T(8,128)}, f32[168,128]{1,0:T(8,128)S(1)}, u32[]{:S(2)}, u32[]{:S(2)}) collective-permute-start(f32[168,128]{1,0:T(8,128)} %get-tuple-element.16), channel_id=1, source_target_pairs={{0,4},{4,0},{1,5},{5,1},{2,6},{6,2},{3,7},{7,3},{8,12},{12,8},{9,1... | collective-permute-start | bytes 258056 | tf_op jit(solution)/shard_map/ppermute | solution.py:465
  10.4 3.4 %copy-start = (f32[168,128]{1,0:T(8,128)S(1)}, f32[168,128]{1,0:T(8,128)}, u32[]{:S(2)}) copy-start(f32[168,128]{1,0:T(8,128)} %get-tuple-element.15.own) | copy-start | bytes 258052
  14.3 24.7 %copy-start.1 = (f32[70,256]{1,0:T(8,128)S(1)}, f32[70,256]{1,0:T(8,128)}, u32[]{:S(2)}) copy-start(f32[70,256]{1,0:T(8,128)} %init_ref) | copy-start | bytes 215044
  14.3 24.7 %copy-start.2 = (f32[40,8]{1,0:T(8,128)S(1)}, f32[40,8]{1,0:T(8,128)}, u32[]{:S(2)}) copy-start(f32[40,8]{1,0:T(8,128)} %get-tuple-element.23.par) | copy-start | bytes 3844
  142.8 3.9 %collective-permute-start.2 = (f32[168,128]{1,0:T(8,128)S(1)}, f32[168,128]{1,0:T(8,128)S(1)}, u32[]{:S(2)}, u32[]{:S(2)}) collective-permute-start(f32[168,128]{1,0:T(8,128)S(1)} %get-tuple-element.25), channel_id=1, source_target_pairs={{0,4},{4,0},{1,5},{5,1},{2,6},{6,2},{3,7},{7,3},{8,12},{12,8},{9,1... | collective-permute-start | bytes 258056 | tf_op jit(solution)/shard_map/ppermute | solution.py:465

commit v5 on v4

--- a/solution.py
+++ b/solution.py
@@ -20,6 +20,8 @@
 STEPS = GROUP * HS
 LANES = 128
 ENV = 1024
+MAIN = 32
+DENSE = BLOCKS * MAIN + 16
 TM = ("x", "z", "c")
 PEERS = ("x", "z")
 
@@ -70,6 +72,20 @@
         )
         for c in range(4)
     ]
+
+
+def fine_row(e, i):
+    return e * MAIN + i if i < MAIN else BLOCKS * MAIN + 4 * e + i - MAIN
+
+
+def put_fine(ref, e, part):
+    ref[e * MAIN : (e + 1) * MAIN, :] = part[:MAIN]
+    ref[fine_row(e, MAIN) : fine_row(e, MAIN) + DOF - MAIN, :] = part[MAIN:DOF]
+
+
+def get_fine(ref, e):
+    tail = ref[fine_row(e, MAIN) : fine_row(e, MAIN) + DOF - MAIN, :]
+    return jnp.concatenate([ref[e * MAIN : (e + 1) * MAIN, :], tail])
 
 
 def shifted(value, by):
@@ -148,7 +164,7 @@
 
 
 def main_kernel(
-    chip, init_ref, recv, par, out, rows, fold, mb, ma, wide, cols, tau_b, stiff_b, damp_b, spring, fric, start, end, shift, pos, vel, force, vec, corr
+    chip, init_ref, recv, par, out, rows, fold, mb, ma, mx, wide, cols, tau_b, stiff_b, damp_b, grav, spring, fric, start, end, shift, pos, vel, force, vec, corr
 ):
     for c in range(3):
         rows[c * LANES : (c + 1) * LANES, :] = jnp.concatenate(
@@ -173,6 +189,9 @@
 
     def place_mass(n, carry):
         for k in range(5):
+            mx[5 * n + k] = jnp.zeros((8, LANES), f32)
+            for half in (0, 4):
+                mx[5 * n + k, half : half + DOF - MAIN, :] = mb[5 * n + k, MAIN:DOF, :]
             for b, spread in enumerate(block_spread(mb[5 * n + k])):
                 ma[b, 5 * n + k] = spread
         return carry
@@ -185,17 +204,18 @@
         spring[t] = (stiffness + gravity + here * contact_stiffness) * (FINE * DT)
         fric[t] = (damping + here * contact_damping) * DT
 
+    for ref in (tau_b, stiff_b, damp_b, grav, shift, pos, vel):
+        ref[...] = jnp.zeros_like(ref)
     for j in range(HS):
         turned = block_transpose([rows[(2 * b + j) * PAD : (2 * b + j + 1) * PAD, :] for b in range(GROUP)])
         touch = block_transpose(
             [rows[ROW_CONTACT + 2 * b + j : ROW_CONTACT + 2 * b + j + 1, :] for b in range(GROUP)]
         )
         for e in range(BLOCKS):
-            tau_b[j, e] = turned[e] * (FINE * FINE * TURN)
-            stiff_b[j, e] = (stiffness + touch[e] * contact_stiffness) * (FINE * FINE)
-            damp_b[j, e] = (damping + touch[e] * contact_damping) * FINE
-
-    grav = gravity * (FINE * FINE * TURN)
+            put_fine(tau_b.at[j], e, turned[e] * (FINE * FINE * TURN))
+            put_fine(stiff_b.at[j], e, (stiffness + touch[e] * contact_stiffness) * (FINE * FINE))
+            put_fine(damp_b.at[j], e, (damping + touch[e] * contact_damping) * FINE)
+            put_fine(grav, e, gravity * (FINE * FINE * TURN))
 
     def half_step(b, t, states, driven):
         moved = []
@@ -272,13 +292,22 @@
         lax.fori_loop(0, 6, some, 0)
 
     def more_columns(level):
-        def one(cg, carry):
-            low, high = apply_wide(level - 1, lambda r: cols[cg, r : r + 1, :])
-            cols[cg, :PAD, :] = low
-            cols[cg, PAD:, :] = high
+        def two(pair, carry):
+            totals = [None] * 4
+            for k in range(2 * DOF):
+                at = state_row(k)
+                parts = (wide[level - 1, k, :PAD, :], wide[level - 1, k, PAD:, :])
+                for n in range(2):
+                    row = cols[2 * pair + n, at : at + 1, :]
+                    for h in range(2):
+                        term = parts[h] * row
+                        totals[2 * n + h] = term if k == 0 else totals[2 * n + h] + term
+            for n in range(2):
+                cols[2 * pair + n, :PAD, :] = totals[2 * n]
+                cols[2 * pair + n, PAD:, :] = totals[2 * n + 1]
             return carry
 
-        lax.fori_loop(0, 18, one, 0)
+        lax.fori_loop(0, 9, two, 0)
 
     spread_columns(0, 1)
     more_columns(1)
@@ -324,37 +353,49 @@
     lax.fori_loop(0, GROUP, driven_keep, entry)
 
     corr[...] = jnp.zeros_like(corr)
+    upper = lax.broadcasted_iota(jnp.int32, (8, LANES), 0) < 4
 
     def iteration(it, carry):
         for half, ref in ((0, pos), (PAD, vel)):
-            for e, part in enumerate(block_transpose([start[b, half : half + PAD, :] for b in range(GROUP)])):
-                ref[e] = part
+            for e, part in enumerate(block_transpose([start[b, half : half + DOF, :] for b in range(GROUP)])):
+                put_fine(ref, e, part)
 
         def substep(n, carry):
+            for u in range(4):
+                substep_one(n * 4 + u)
+            return carry
+
+        def substep_one(n):
             j = n // SUB
-            for e in range(BLOCKS):
-                p = pos[e]
+            for v in range(DENSE // 8):
+                at = slice(8 * v, 8 * v + 8)
+                p = pos[at, :]
                 f = p - jnp.round(p)
                 s = f * f
                 poly = SINE[4] * s + SINE[3]
                 for coef in (SINE[2], SINE[1], SINE[0]):
                     poly = poly * s + coef
                 sine = (f * (0.25 - s)) * poly
-                force[e] = tau_b[j, e] - stiff_b[j, e] * p - damp_b[j, e] * vel[e] - grav * sine
-            acc = [vel[e] for e in range(BLOCKS)]
+                pull = tau_b[j, at, :] - stiff_b[j, at, :] * p - damp_b[j, at, :] * vel[at, :] - grav[at, :] * sine
+                force[at, :] = pull
+            acc = [vel[e * MAIN : (e + 1) * MAIN, :] for e in range(BLOCKS)]
+            tail = [vel[BLOCKS * MAIN + 8 * n : BLOCKS * MAIN + 8 * n + 8, :] for n in range(2)]
             for k in range(DOF):
-                mass = mb[k]
+                mass = mb[k, :MAIN, :]
+                rest = mx[k]
+                row = [force[fine_row(e, k) : fine_row(e, k) + 1, :] for e in range(BLOCKS)]
                 for e in range(BLOCKS):
-                    acc[e] = acc[e] + mass * force[e, k : k + 1, :]
-            for e in range(BLOCKS):
-                vel[e] = acc[e]
-                pos[e] = pos[e] + acc[e]
-            return carry
-
-        lax.fori_loop(0, HS * SUB, substep, 0)
+                    acc[e] = acc[e] + mass * row[e]
+                for n in range(2):
+                    tail[n] = tail[n] + rest * jnp.where(upper, row[2 * n], row[2 * n + 1])
+            now = jnp.concatenate(acc + tail)
+            vel[...] = now
+            pos[...] = pos[...] + now
+
+        lax.fori_loop(0, HS * SUB // 4, substep, 0)
         for half, ref in ((0, pos), (PAD, vel)):
-            for b, part in enumerate(block_transpose([ref[e] for e in range(BLOCKS)])):
-                shift[b, half : half + PAD, :] = part - end[b, half : half + PAD, :]
+            for b, part in enumerate(block_transpose([get_fine(ref, e) for e in range(BLOCKS)])):
+                shift[b, half : half + DOF, :] = part - end[b, half : half + DOF, :]
 
         def chain(b, qw):
             q, w = one_slice(b, qw[0], qw[1], False)
@@ -442,19 +483,21 @@
         (FOLD, LANES),
         (DOF, *tile),
         (GROUP, DOF, *tile),
+        (DOF, 8, LANES),
         (3, 72, 2 * PAD, LANES),
         (18, 2 * PAD, LANES),
-        (HS, BLOCKS, *tile),
-        (HS, BLOCKS, *tile),
-        (HS, BLOCKS, *tile),
+        (HS, DENSE, LANES),
+        (HS, DENSE, LANES),
+        (HS, DENSE, LANES),
+        (DENSE, LANES),
         (STEPS, *tile),
         (STEPS, *tile),
         (GROUP, 2 * PAD, LANES),
         (GROUP, 2 * PAD, LANES),
         (GROUP, 2 * PAD, LANES),
-        (BLOCKS, *tile),
-        (BLOCKS, *tile),
-        (BLOCKS, *tile),
+        (DENSE, LANES),
+        (DENSE, LANES),
+        (DENSE, LANES),
         (2, 2 * PAD, LANES),
         (8, LANES),
     ]

time: 148 us -> 144 us (0.973)
  Pallas kernels: 89.5 us -> 85.4 us
    pallas_call x4, Pallas kernels: 87.7 us -> 83.7 us  [local_call(): pl.pallas_call(kernel, in_specs=[smem] + [vmem] * len(arrays), out_specs=...]
where the time goes in v5:
time: 144 us; the launch traced here: 143 us
  Pallas kernels  85.4 us (59%)
  blocking collectives  42 us (29%)
  starting transfers between devices  9.91 us (7%)
  waiting for transfers between devices  4.67 us (3%)
    pallas_call x4, Pallas kernels, local_call(): pl.pallas_call(kernel, in_specs=[smem] + [vmem] * len(arrays), out_specs=...  83.7 us
    all_to_all x2, blocking collectives, exchanged(): return lax.all_to_all(value, PEERS, split_axis=0, concat_axis=0, tiled=True)  42 us
    all_to_all x1, starting transfers between devices, shards(): lax.all_to_all(counts, ('c', 'y'), split_axis=0, concat_axis=0, tiled=True)  6.47 us
    ppermute x3, starting transfers between devices, swapped(): return lax.ppermute(value, 'c', [(0, 1), (1, 0)])  3.44 us
    all_to_all x1, waiting for transfers between devices, shards(): lax.all_to_all(counts, ('c', 'y'), split_axis=0, concat_axis=0, tiled=True)  3.12 us
  transfers between devices with their start and end apart: 4, of which 3 were waited for; matrix products, arithmetic and copies ran while one was open for 0% of the time, Pallas kernels for 0%

profile of v5, /device:TPU:1, one launch (start us, length us, event | category | flops | bytes accessed | tf_op | source)
XLA Modules:
  0.0 143.3 jit_solution(12692170352907841543)
XLA Ops:
  0.6 1.7 %split.1 = (f32[8,4,128]{2,1,0:T(4,128)}, f32[40,8]{1,0:T(8,128)}, f32[35,2,35]{2,1,0:T(2,128)}, f32[168,128]{1,0:T(8,128)}, f32[168,128]{1,0:T(8,128)}) custom-call(s32[1]{0:T(128)} %bitcast.core, s32[4,256]{1,0:T(4,128)} %contact.1, f32[35,4,256]{2,1,0:T(4,128)} %bitcast.18, f32[35,2,35]{2,1,0:T(2,128)} %bitcast.19, f32[1,35]{1,0:T(1,128)} %bitcast.20, ...), custom_call_target="tpu_custom_call" | custom-call | tf_op jit(solution)/shard_map/split/pallas_call | solution.py:532
  2.4 0.0 copy-start.3
  2.4 6.5 %all-to-all-start = ((f32[8,4,128]{2,1,0:T(4,128)}), f32[8,4,128]{2,1,0:T(4,128)S(1)}, u32[]{:S(2)}, u32[]{:S(2)}) async-start(f32[8,4,128]{2,1,0:T(4,128)} %get-tuple-element.17), calls=%async_computation | async-start | bytes 32768 | tf_op jit(solution)/shard_map/all_to_all | solution.py:554
  8.9 0.0 copy-done.3
  8.9 0.2 collective-permute-start.1
  9.1 0.3 collective-permute-start
  9.4 0.1 pad_add_fusion.chip
  9.5 0.6 collective-permute-done.1
  10.1 0.1 fusion
  10.2 0.1 rev.3
  10.3 0.1 fusion.1
  10.4 0.0 copy-start
  10.4 0.1 reshape.18
  10.6 0.1 copy.14
  10.6 3.1 %all-to-all-done = f32[8,4,128]{2,1,0:T(4,128)S(1)} async-done(((f32[8,4,128]{2,1,0:T(4,128)}), f32[8,4,128]{2,1,0:T(4,128)S(1)}, u32[]{:S(2)}, u32[]{:S(2)}) %all-to-all-start) | async-done | bytes 16416 | tf_op jit(solution)/shard_map/all_to_all | solution.py:554
  13.8 0.0 collective-permute-done.back
  13.8 0.0 copy-done
  13.8 0.5 pack.1
  14.3 0.0 copy-start.1
  14.3 0.0 copy-start.2
  14.3 24.7 %all_to_all.15.recv = f32[32,32,128]{2,1,0:T(8,128)S(1)} all-to-all(f32[32,32,128]{2,1,0:T(8,128)S(1)} %pack.1), channel_id=1, replica_groups=mesh['x'=4,'z'=8,'c'=2,'y'=4] {'x','z'}, dimensions={0} | all-to-all | bytes 1048576 | tf_op jit(solution)/shard_map/all_to_all | solution.py:512
  39.0 0.0 copy-done.1
  39.0 0.0 copy-done.2
  39.0 82.3 %parareal.1 = f32[32,3,4,128]{3,2,1,0:T(4,128)S(1)} custom-call(s32[2]{0:T(128)S(1)} %pad_add_fusion.chip, f32[70,256]{1,0:T(8,128)S(1)} %copy-done.1, f32[32,32,128]{2,1,0:T(8,128)S(1)} %all_to_all.15.recv, f32[40,8]{1,0:T(8,128)S(1)} %copy-done.2), custom_call_target="tpu_custom_call" | custom-call | tf_op jit(solution)/shard_map/parareal/pallas_call | solution.py:468
  121.3 17.3 %all_to_all.16.recv = f32[32,3,4,128]{3,2,1,0:T(4,128)S(1)} all-to-all(f32[32,3,4,128]{3,2,1,0:T(4,128)S(1)} %parareal.1), channel_id=1, replica_groups=mesh['x'=4,'z'=8,'c'=2,'y'=4] {'x','z'}, dimensions={0} | all-to-all | bytes 393216 | tf_op jit(solution)/shard_map/all_to_all | solution.py:512
  138.5 0.2 unpack.1
  138.7 2.9 %collective-permute-start.2 = (f32[168,128]{1,0:T(8,128)S(1)}, f32[168,128]{1,0:T(8,128)S(1)}, u32[]{:S(2)}, u32[]{:S(2)}) collective-permute-start(f32[168,128]{1,0:T(8,128)S(1)} %get-tuple-element.25), channel_id=1, source_target_pairs={{0,4},{4,0},{1,5},{5,1},{2,6},{6,2},{3,7},{7,3},{8,12},{12,8},{9,1... | collective-permute-start | bytes 258056 | tf_op jit(solution)/shard_map/ppermute | solution.py:508
  141.7 0.9 collective-permute-done.2.back
  142.6 0.7 join.1
  (6 shorter events, 0.0 us)
Async XLA Ops:
  2.4 6.5 %copy-start.3 = (f32[35,2,35]{2,1,0:T(2,128)S(1)}, f32[35,2,35]{2,1,0:T(2,128)}, u32[]{:S(2)}) copy-start(f32[35,2,35]{2,1,0:T(2,128)} %get-tuple-element.18) | copy-start | bytes 29404
  2.4 11.4 %all-to-all-start = ((f32[8,4,128]{2,1,0:T(4,128)}), f32[8,4,128]{2,1,0:T(4,128)S(1)}, u32[]{:S(2)}, u32[]{:S(2)}) async-start(f32[8,4,128]{2,1,0:T(4,128)} %get-tuple-element.17), calls=%async_computation | async-start | bytes 32768 | tf_op jit(solution)/shard_map/all_to_all | solution.py:554
  8.9 1.2 collective-permute-start.1
  9.1 4.7 %collective-permute-start = (f32[168,128]{1,0:T(8,128)}, f32[168,128]{1,0:T(8,128)S(1)}, u32[]{:S(2)}, u32[]{:S(2)}) collective-permute-start(f32[168,128]{1,0:T(8,128)} %get-tuple-element.16), channel_id=1, source_target_pairs={{0,4},{4,0},{1,5},{5,1},{2,6},{6,2},{3,7},{7,3},{8,12},{12,8},{9,1... | collective-permute-start | bytes 258056 | tf_op jit(solution)/shard_map/ppermute | solution.py:508
  10.4 3.4 %copy-start = (f32[168,128]{1,0:T(8,128)S(1)}, f32[168,128]{1,0:T(8,128)}, u32[]{:S(2)}) copy-start(f32[168,128]{1,0:T(8,128)} %get-tuple-element.15.own) | copy-start | bytes 258052
  14.3 24.7 %copy-start.1 = (f32[70,256]{1,0:T(8,128)S(1)}, f32[70,256]{1,0:T(8,128)}, u32[]{:S(2)}) copy-start(f32[70,256]{1,0:T(8,128)} %init_ref) | copy-start | bytes 215044
  14.3 24.7 %copy-start.2 = (f32[40,8]{1,0:T(8,128)S(1)}, f32[40,8]{1,0:T(8,128)}, u32[]{:S(2)}) copy-start(f32[40,8]{1,0:T(8,128)} %get-tuple-element.23.par) | copy-start | bytes 3844
  138.7 3.9 %collective-permute-start.2 = (f32[168,128]{1,0:T(8,128)S(1)}, f32[168,128]{1,0:T(8,128)S(1)}, u32[]{:S(2)}, u32[]{:S(2)}) collective-permute-start(f32[168,128]{1,0:T(8,128)S(1)} %get-tuple-element.25), channel_id=1, source_target_pairs={{0,4},{4,0},{1,5},{5,1},{2,6},{6,2},{3,7},{7,3},{8,12},{12,8},{9,1... | collective-permute-start | bytes 258056 | tf_op jit(solution)/shard_map/ppermute | solution.py:508

commit v6 on v5

--- a/solution.py
+++ b/solution.py
@@ -22,6 +22,8 @@
 ENV = 1024
 MAIN = 32
 DENSE = BLOCKS * MAIN + 16
+STATE = 2 * DOF
+ROWS = 72
 TM = ("x", "z", "c")
 PEERS = ("x", "z")
 
@@ -159,12 +161,8 @@
         out[:, IN_ROWS + m, :] = jnp.broadcast_to(mass[m : m + 1, :], (CHIPS, LANES))
 
 
-def state_row(k):
-    return k if k < DOF else k + PAD - DOF
-
-
 def main_kernel(
-    chip, init_ref, recv, par, out, rows, fold, mb, ma, mx, wide, cols, tau_b, stiff_b, damp_b, grav, spring, fric, start, end, shift, pos, vel, force, vec, corr
+    chip, init_ref, recv, par, out, rows, fold, mb, ma, mx, wide, cols, tau_b, stiff_b, damp_b, grav, spring, fric, start, end, shift, diff, pos, vel, force, vec, corr
 ):
     for c in range(3):
         rows[c * LANES : (c + 1) * LANES, :] = jnp.concatenate(
@@ -239,17 +237,17 @@
     def one_slice(b, q, w, driven):
         return slice_step(b, ((q, w),), driven)[0]
 
-    def apply_wide(level, row_of):
+    def apply_wide(level, slot):
         low = high = None
-        for k in range(2 * DOF):
-            row = row_of(state_row(k))
+        for k in range(STATE):
+            row = vec[slot, k : k + 1, :]
             term = wide[level, k, :PAD, :] * row
             low = term if low is None else low + term
-            if k < DOF:
+            if k < PAD:
                 term = wide[level, k, PAD:, :] * row
                 high = term if high is None else high + term
-        for k in range(DOF, 2 * DOF):
-            high = high + wide[level, k, PAD:, :] * row_of(state_row(k))
+        for k in range(PAD, STATE):
+            high = high + wide[level, k, PAD:, :] * vec[slot, k : k + 1, :]
         return low, high
 
     row80 = lax.broadcasted_iota(jnp.int32, (2 * PAD, LANES), 0)
@@ -273,8 +271,9 @@
         states = half_step(0, 1, states, False)
         states = lax.fori_loop(1, GROUP, lambda b, now: slice_step(b, now, False), states)
         for n in range(2):
-            cols[2 * pair + n, :PAD, :] = states[n][0]
-            cols[2 * pair + n, PAD:, :] = states[n][1]
+            cols[2 * pair + n, :DOF, :] = states[n][0][:DOF]
+            cols[2 * pair + n, DOF:STATE, :] = states[n][1][:DOF]
+            cols[2 * pair + n, STATE:, :] = jnp.zeros((ROWS - STATE, LANES), f32)
         return carry
 
     lax.fori_loop(0, 9, first_columns, 0)
@@ -294,11 +293,10 @@
     def more_columns(level):
         def two(pair, carry):
             totals = [None] * 4
-            for k in range(2 * DOF):
-                at = state_row(k)
+            for k in range(STATE):
                 parts = (wide[level - 1, k, :PAD, :], wide[level - 1, k, PAD:, :])
                 for n in range(2):
-                    row = cols[2 * pair + n, at : at + 1, :]
+                    row = cols[2 * pair + n, k : k + 1, :]
                     for h in range(2):
                         term = parts[h] * row
                         totals[2 * n + h] = term if k == 0 else totals[2 * n + h] + term
@@ -316,18 +314,38 @@
     spread_columns(2, 0)
 
     def scan_groups(q, w):
-        def add_earlier(level, by, slot, base, state):
+        def add_earlier(level, by, slot, state):
             vec[slot, :PAD, :] = shifted(state[0], by)
-            vec[slot, PAD:, :] = shifted(state[1], by)
-            low, high = apply_wide(level, lambda r: vec[slot, r : r + 1, :])
-            return base[0] + low, base[1] + high
-
-        state = (q, w)
-        state = add_earlier(0, 1, 0, state, state)
-        state = base = add_earlier(1, 2, 1, state, state)
-        for n in range(7):
-            state = add_earlier(2, 4, n % 2, base, state)
-        return state
+            vec[slot, PAD:ROWS, :] = shifted(state[1], by)
+            low, high = apply_wide(level, slot)
+            return state[0] + low, state[1] + high
+
+        diff[:DOF, :] = q[:DOF]
+        diff[DOF:STATE, :] = w[:DOF]
+        diff[STATE:, :] = jnp.zeros((2 * PAD - STATE, LANES), f32)
+        base = diff[:PAD, :], diff[PAD:ROWS, :]
+        base = add_earlier(0, 1, 0, base)
+        base = add_earlier(1, 2, 1, base)
+        diff[:PAD, :], diff[PAD:ROWS, :] = base
+        vec[0, :PAD, :] = shifted(base[0], 4)
+
+        def more(n, now):
+            vec[0, PAD:ROWS, :] = shifted(now[1], 4)
+            low, high = diff[:PAD, :], diff[PAD:ROWS, :]
+            for k in range(PAD):
+                row = vec[0, k : k + 1, :]
+                low = low + wide[2, k, :PAD, :] * row
+                high = high + wide[2, k, PAD:, :] * row
+            for k in range(PAD, STATE):
+                low = low + wide[2, k, :PAD, :] * vec[0, k : k + 1, :]
+            vec[0, :PAD, :] = shifted(low, 4)
+            for k in range(PAD, STATE):
+                high = high + wide[2, k, PAD:, :] * vec[0, k : k + 1, :]
+            return low, high
+
+        diff[:PAD, :], diff[PAD:ROWS, :] = lax.fori_loop(0, 7, more, base)
+        used = lax.broadcasted_iota(jnp.int32, (PAD, LANES), 0) < DOF
+        return jnp.where(used, diff[:PAD, :], 0.0), jnp.where(used, diff[DOF : DOF + PAD, :], 0.0)
 
     first = (lane_index(2 * PAD) & 31) == 0
     back_by = LANES - chip[0]
@@ -484,8 +502,8 @@
         (DOF, *tile),
         (GROUP, DOF, *tile),
         (DOF, 8, LANES),
-        (3, 72, 2 * PAD, LANES),
-        (18, 2 * PAD, LANES),
+        (3, 72, ROWS, LANES),
+        (18, ROWS, LANES),
         (HS, DENSE, LANES),
         (HS, DENSE, LANES),
         (HS, DENSE, LANES),
@@ -495,6 +513,7 @@
         (GROUP, 2 * PAD, LANES),
         (GROUP, 2 * PAD, LANES),
         (GROUP, 2 * PAD, LANES),
+        (2 * PAD, LANES),
         (DENSE, LANES),
         (DENSE, LANES),
         (DENSE, LANES),

time: 144 us -> 142 us (0.986)
  no operation moved by 1% of the time
where the time goes in v6:
time: 142 us
  Pallas kernels  84 us (59%)
  blocking collectives  42 us (30%)
  starting transfers between devices  9.91 us (7%)
  waiting for transfers between devices  4.67 us (3%)
    pallas_call x4, Pallas kernels, local_call(): pl.pallas_call(kernel, in_specs=[smem] + [vmem] * len(arrays), out_specs=...  82.3 us
    all_to_all x2, blocking collectives, exchanged(): return lax.all_to_all(value, PEERS, split_axis=0, concat_axis=0, tiled=True)  42 us
    all_to_all x1, starting transfers between devices, shards(): lax.all_to_all(counts, ('c', 'y'), split_axis=0, concat_axis=0, tiled=True)  6.47 us
    ppermute x3, starting transfers between devices, swapped(): return lax.ppermute(value, 'c', [(0, 1), (1, 0)])  3.44 us
    all_to_all x1, waiting for transfers between devices, shards(): lax.all_to_all(counts, ('c', 'y'), split_axis=0, concat_axis=0, tiled=True)  3.12 us
  transfers between devices with their start and end apart: 4, of which 3 were waited for; matrix products, arithmetic and copies ran while one was open for 0% of the time, Pallas kernels for 0%

profile of v6, /device:TPU:1, one launch (start us, length us, event | category | flops | bytes accessed | tf_op | source)
XLA Modules:
  0.0 141.9 jit_solution(12666724037045028001)
XLA Ops:
  0.6 1.7 %split.1 = (f32[8,4,128]{2,1,0:T(4,128)}, f32[40,8]{1,0:T(8,128)}, f32[35,2,35]{2,1,0:T(2,128)}, f32[168,128]{1,0:T(8,128)}, f32[168,128]{1,0:T(8,128)}) custom-call(s32[1]{0:T(128)} %bitcast.core, s32[4,256]{1,0:T(4,128)} %contact.1, f32[35,4,256]{2,1,0:T(4,128)} %bitcast.18, f32[35,2,35]{2,1,0:T(2,128)} %bitcast.19, f32[1,35]{1,0:T(1,128)} %bitcast.20, ...), custom_call_target="tpu_custom_call" | custom-call | tf_op jit(solution)/shard_map/split/pallas_call | solution.py:551
  2.4 0.0 copy-start.3
  2.4 6.5 %all-to-all-start = ((f32[8,4,128]{2,1,0:T(4,128)}), f32[8,4,128]{2,1,0:T(4,128)S(1)}, u32[]{:S(2)}, u32[]{:S(2)}) async-start(f32[8,4,128]{2,1,0:T(4,128)} %get-tuple-element.17), calls=%async_computation | async-start | bytes 32768 | tf_op jit(solution)/shard_map/all_to_all | solution.py:573
  8.9 0.0 copy-done.3
  8.9 0.2 collective-permute-start.1
  9.1 0.3 collective-permute-start
  9.4 0.1 pad_add_fusion.chip
  9.5 0.6 collective-permute-done.1
  10.1 0.1 fusion
  10.2 0.1 rev.3
  10.3 0.1 fusion.1
  10.4 0.0 copy-start
  10.4 0.1 reshape.18
  10.6 0.1 copy.14
  10.6 3.1 %all-to-all-done = f32[8,4,128]{2,1,0:T(4,128)S(1)} async-done(((f32[8,4,128]{2,1,0:T(4,128)}), f32[8,4,128]{2,1,0:T(4,128)S(1)}, u32[]{:S(2)}, u32[]{:S(2)}) %all-to-all-start) | async-done | bytes 16416 | tf_op jit(solution)/shard_map/all_to_all | solution.py:573
  13.8 0.0 collective-permute-done.back
  13.8 0.0 copy-done
  13.8 0.5 pack.1
  14.3 0.0 copy-start.1
  14.3 0.0 copy-start.2
  14.3 24.7 %all_to_all.15.recv = f32[32,32,128]{2,1,0:T(8,128)S(1)} all-to-all(f32[32,32,128]{2,1,0:T(8,128)S(1)} %pack.1), channel_id=1, replica_groups=mesh['x'=4,'z'=8,'c'=2,'y'=4] {'x','z'}, dimensions={0} | all-to-all | bytes 1048576 | tf_op jit(solution)/shard_map/all_to_all | solution.py:531
  39.0 0.0 copy-done.1
  39.0 0.0 copy-done.2
  39.0 80.9 %parareal.1 = f32[32,3,4,128]{3,2,1,0:T(4,128)S(1)} custom-call(s32[2]{0:T(128)S(1)} %pad_add_fusion.chip, f32[70,256]{1,0:T(8,128)S(1)} %copy-done.1, f32[32,32,128]{2,1,0:T(8,128)S(1)} %all_to_all.15.recv, f32[40,8]{1,0:T(8,128)S(1)} %copy-done.2), custom_call_target="tpu_custom_call" | custom-call | tf_op jit(solution)/shard_map/parareal/pallas_call | solution.py:486
  119.9 17.3 %all_to_all.16.recv = f32[32,3,4,128]{3,2,1,0:T(4,128)S(1)} all-to-all(f32[32,3,4,128]{3,2,1,0:T(4,128)S(1)} %parareal.1), channel_id=1, replica_groups=mesh['x'=4,'z'=8,'c'=2,'y'=4] {'x','z'}, dimensions={0} | all-to-all | bytes 393216 | tf_op jit(solution)/shard_map/all_to_all | solution.py:531
  137.2 0.2 unpack.1
  137.3 2.9 %collective-permute-start.2 = (f32[168,128]{1,0:T(8,128)S(1)}, f32[168,128]{1,0:T(8,128)S(1)}, u32[]{:S(2)}, u32[]{:S(2)}) collective-permute-start(f32[168,128]{1,0:T(8,128)S(1)} %get-tuple-element.25), channel_id=1, source_target_pairs={{0,4},{4,0},{1,5},{5,1},{2,6},{6,2},{3,7},{7,3},{8,12},{12,8},{9,1... | collective-permute-start | bytes 258056 | tf_op jit(solution)/shard_map/ppermute | solution.py:527
  140.3 0.9 collective-permute-done.2.back
  141.2 0.7 join.1
  (6 shorter events, 0.0 us)
Async XLA Ops:
  2.4 6.5 %copy-start.3 = (f32[35,2,35]{2,1,0:T(2,128)S(1)}, f32[35,2,35]{2,1,0:T(2,128)}, u32[]{:S(2)}) copy-start(f32[35,2,35]{2,1,0:T(2,128)} %get-tuple-element.18) | copy-start | bytes 29404
  2.4 11.4 %all-to-all-start = ((f32[8,4,128]{2,1,0:T(4,128)}), f32[8,4,128]{2,1,0:T(4,128)S(1)}, u32[]{:S(2)}, u32[]{:S(2)}) async-start(f32[8,4,128]{2,1,0:T(4,128)} %get-tuple-element.17), calls=%async_computation | async-start | bytes 32768 | tf_op jit(solution)/shard_map/all_to_all | solution.py:573
  8.9 1.2 collective-permute-start.1
  9.1 4.7 %collective-permute-start = (f32[168,128]{1,0:T(8,128)}, f32[168,128]{1,0:T(8,128)S(1)}, u32[]{:S(2)}, u32[]{:S(2)}) collective-permute-start(f32[168,128]{1,0:T(8,128)} %get-tuple-element.16), channel_id=1, source_target_pairs={{0,4},{4,0},{1,5},{5,1},{2,6},{6,2},{3,7},{7,3},{8,12},{12,8},{9,1... | collective-permute-start | bytes 258056 | tf_op jit(solution)/shard_map/ppermute | solution.py:527
  10.4 3.4 %copy-start = (f32[168,128]{1,0:T(8,128)S(1)}, f32[168,128]{1,0:T(8,128)}, u32[]{:S(2)}) copy-start(f32[168,128]{1,0:T(8,128)} %get-tuple-element.15.own) | copy-start | bytes 258052
  14.3 24.7 %copy-start.1 = (f32[70,256]{1,0:T(8,128)S(1)}, f32[70,256]{1,0:T(8,128)}, u32[]{:S(2)}) copy-start(f32[70,256]{1,0:T(8,128)} %init_ref) | copy-start | bytes 215044
  14.3 24.7 %copy-start.2 = (f32[40,8]{1,0:T(8,128)S(1)}, f32[40,8]{1,0:T(8,128)}, u32[]{:S(2)}) copy-start(f32[40,8]{1,0:T(8,128)} %get-tuple-element.23.par) | copy-start | bytes 3844
  137.3 3.9 %collective-permute-start.2 = (f32[168,128]{1,0:T(8,128)S(1)}, f32[168,128]{1,0:T(8,128)S(1)}, u32[]{:S(2)}, u32[]{:S(2)}) collective-permute-start(f32[168,128]{1,0:T(8,128)S(1)} %get-tuple-element.25), channel_id=1, source_target_pairs={{0,4},{4,0},{1,5},{5,1},{2,6},{6,2},{3,7},{7,3},{8,12},{12,8},{9,1... | collective-permute-start | bytes 258056 | tf_op jit(solution)/shard_map/ppermute | solution.py:527

commit v7 on v6

--- a/solution.py
+++ b/solution.py
@@ -88,6 +88,12 @@
 def get_fine(ref, e):
     tail = ref[fine_row(e, MAIN) : fine_row(e, MAIN) + DOF - MAIN, :]
     return jnp.concatenate([ref[e * MAIN : (e + 1) * MAIN, :], tail])
+
+
+def unrolled(first, last, body, state):
+    for b in range(first, last):
+        state = body(b, state)
+    return state
 
 
 def shifted(value, by):
@@ -269,7 +275,7 @@
             unit = jnp.where(row80 == col, 1.0, 0.0)
             states.append(first_half(4 * (2 * pair + n), unit[:PAD], unit[PAD:]))
         states = half_step(0, 1, states, False)
-        states = lax.fori_loop(1, GROUP, lambda b, now: slice_step(b, now, False), states)
+        states = unrolled(1, GROUP, lambda b, now: slice_step(b, now, False), states)
         for n in range(2):
             cols[2 * pair + n, :DOF, :] = states[n][0][:DOF]
             cols[2 * pair + n, DOF:STATE, :] = states[n][1][:DOF]
@@ -379,8 +385,8 @@
                 put_fine(ref, e, part)
 
         def substep(n, carry):
-            for u in range(4):
-                substep_one(n * 4 + u)
+            for u in range(8):
+                substep_one(n * 8 + u)
             return carry
 
         def substep_one(n):
@@ -410,7 +416,7 @@
             vel[...] = now
             pos[...] = pos[...] + now
 
-        lax.fori_loop(0, HS * SUB // 4, substep, 0)
+        lax.fori_loop(0, HS * SUB // 8, substep, 0)
         for half, ref in ((0, pos), (PAD, vel)):
             for b, part in enumerate(block_transpose([get_fine(ref, e) for e in range(BLOCKS)])):
                 shift[b, half : half + DOF, :] = part - end[b, half : half + DOF, :]
@@ -419,7 +425,7 @@
             q, w = one_slice(b, qw[0], qw[1], False)
             return q + shift[b, :PAD, :], w + shift[b, PAD:, :]
 
-        q, w = lax.fori_loop(1, GROUP, chain, (shift[0, :PAD, :], shift[0, PAD:, :]))
+        q, w = unrolled(1, GROUP, chain, (shift[0, :PAD, :], shift[0, PAD:, :]))
         q, w = scan_groups(q, w)
 
         def keep(b, state):
@@ -434,7 +440,7 @@
             square = jnp.sum(dq * dq + dv * dv, axis=0, keepdims=True)
             return q, w, jnp.maximum(largest, square)
 
-        _, _, largest = lax.fori_loop(
+        _, _, largest = unrolled(
             0, GROUP, keep, (shifted(q, 1), shifted(w, 1), jnp.zeros((1, LANES), f32))
         )
         group = lane_index(1) & 31

time: 142 us -> 141 us (level)
  Pallas kernels: 84 us -> 82.4 us
    pallas_call x4, Pallas kernels: 82.3 us -> 80.7 us  [local_call(): pl.pallas_call(kernel, in_specs=[smem] + [vmem] * len(arrays), out_specs=...]
where the time goes in v7:
time: 141 us; the launch traced here: 140 us
  Pallas kernels  82.4 us (58%)
  blocking collectives  42 us (30%)
  starting transfers between devices  9.91 us (7%)
  waiting for transfers between devices  4.67 us (3%)
    pallas_call x4, Pallas kernels, local_call(): pl.pallas_call(kernel, in_specs=[smem] + [vmem] * len(arrays), out_specs=...  80.7 us
    all_to_all x2, blocking collectives, exchanged(): return lax.all_to_all(value, PEERS, split_axis=0, concat_axis=0, tiled=True)  42 us
    all_to_all x1, starting transfers between devices, shards(): lax.all_to_all(counts, ('c', 'y'), split_axis=0, concat_axis=0, tiled=True)  6.47 us
    ppermute x3, starting transfers between devices, swapped(): return lax.ppermute(value, 'c', [(0, 1), (1, 0)])  3.44 us
    all_to_all x1, waiting for transfers between devices, shards(): lax.all_to_all(counts, ('c', 'y'), split_axis=0, concat_axis=0, tiled=True)  3.12 us
  transfers between devices with their start and end apart: 4, of which 3 were waited for; matrix products, arithmetic and copies ran while one was open for 0% of the time, Pallas kernels for 0%

profile of v7, /device:TPU:1, one launch (start us, length us, event | category | flops | bytes accessed | tf_op | source)
XLA Modules:
  0.0 140.3 jit_solution(16922367132529731355)
XLA Ops:
  0.6 1.7 %split.1 = (f32[8,4,128]{2,1,0:T(4,128)}, f32[40,8]{1,0:T(8,128)}, f32[35,2,35]{2,1,0:T(2,128)}, f32[168,128]{1,0:T(8,128)}, f32[168,128]{1,0:T(8,128)}) custom-call(s32[1]{0:T(128)} %bitcast.core, s32[4,256]{1,0:T(4,128)} %contact.1, f32[35,4,256]{2,1,0:T(4,128)} %bitcast.18, f32[35,2,35]{2,1,0:T(2,128)} %bitcast.19, f32[1,35]{1,0:T(1,128)} %bitcast.20, ...), custom_call_target="tpu_custom_call" | custom-call | tf_op jit(solution)/shard_map/split/pallas_call | solution.py:557
  2.4 0.0 copy-start.3
  2.4 6.5 %all-to-all-start = ((f32[8,4,128]{2,1,0:T(4,128)}), f32[8,4,128]{2,1,0:T(4,128)S(1)}, u32[]{:S(2)}, u32[]{:S(2)}) async-start(f32[8,4,128]{2,1,0:T(4,128)} %get-tuple-element.17), calls=%async_computation | async-start | bytes 32768 | tf_op jit(solution)/shard_map/all_to_all | solution.py:579
  8.9 0.0 copy-done.3
  8.9 0.2 collective-permute-start.1
  9.1 0.3 collective-permute-start
  9.4 0.1 pad_add_fusion.chip
  9.5 0.6 collective-permute-done.1
  10.1 0.1 fusion
  10.2 0.1 rev.3
  10.3 0.1 fusion.1
  10.4 0.0 copy-start
  10.4 0.1 reshape.18
  10.6 0.1 copy.14
  10.6 3.1 %all-to-all-done = f32[8,4,128]{2,1,0:T(4,128)S(1)} async-done(((f32[8,4,128]{2,1,0:T(4,128)}), f32[8,4,128]{2,1,0:T(4,128)S(1)}, u32[]{:S(2)}, u32[]{:S(2)}) %all-to-all-start) | async-done | bytes 16416 | tf_op jit(solution)/shard_map/all_to_all | solution.py:579
  13.8 0.0 collective-permute-done.back
  13.8 0.0 copy-done
  13.8 0.5 pack.1
  14.3 0.0 copy-start.1
  14.3 0.0 copy-start.2
  14.3 24.7 %all_to_all.15.recv = f32[32,32,128]{2,1,0:T(8,128)S(1)} all-to-all(f32[32,32,128]{2,1,0:T(8,128)S(1)} %pack.1), channel_id=1, replica_groups=mesh['x'=4,'z'=8,'c'=2,'y'=4] {'x','z'}, dimensions={0} | all-to-all | bytes 1048576 | tf_op jit(solution)/shard_map/all_to_all | solution.py:537
  39.0 0.0 copy-done.1
  39.0 0.0 copy-done.2
  39.0 79.3 %parareal.1 = f32[32,3,4,128]{3,2,1,0:T(4,128)S(1)} custom-call(s32[2]{0:T(128)S(1)} %pad_add_fusion.chip, f32[70,256]{1,0:T(8,128)S(1)} %copy-done.1, f32[32,32,128]{2,1,0:T(8,128)S(1)} %all_to_all.15.recv, f32[40,8]{1,0:T(8,128)S(1)} %copy-done.2), custom_call_target="tpu_custom_call" | custom-call | tf_op jit(solution)/shard_map/parareal/pallas_call | solution.py:492
  118.3 17.3 %all_to_all.16.recv = f32[32,3,4,128]{3,2,1,0:T(4,128)S(1)} all-to-all(f32[32,3,4,128]{3,2,1,0:T(4,128)S(1)} %parareal.1), channel_id=1, replica_groups=mesh['x'=4,'z'=8,'c'=2,'y'=4] {'x','z'}, dimensions={0} | all-to-all | bytes 393216 | tf_op jit(solution)/shard_map/all_to_all | solution.py:537
  135.5 0.2 unpack.1
  135.7 2.9 %collective-permute-start.2 = (f32[168,128]{1,0:T(8,128)S(1)}, f32[168,128]{1,0:T(8,128)S(1)}, u32[]{:S(2)}, u32[]{:S(2)}) collective-permute-start(f32[168,128]{1,0:T(8,128)S(1)} %get-tuple-element.25), channel_id=1, source_target_pairs={{0,4},{4,0},{1,5},{5,1},{2,6},{6,2},{3,7},{7,3},{8,12},{12,8},{9,1... | collective-permute-start | bytes 258056 | tf_op jit(solution)/shard_map/ppermute | solution.py:533
  138.7 0.9 collective-permute-done.2.back
  139.6 0.7 join.1
  (6 shorter events, 0.0 us)
Async XLA Ops:
  2.4 6.5 %copy-start.3 = (f32[35,2,35]{2,1,0:T(2,128)S(1)}, f32[35,2,35]{2,1,0:T(2,128)}, u32[]{:S(2)}) copy-start(f32[35,2,35]{2,1,0:T(2,128)} %get-tuple-element.18) | copy-start | bytes 29404
  2.4 11.4 %all-to-all-start = ((f32[8,4,128]{2,1,0:T(4,128)}), f32[8,4,128]{2,1,0:T(4,128)S(1)}, u32[]{:S(2)}, u32[]{:S(2)}) async-start(f32[8,4,128]{2,1,0:T(4,128)} %get-tuple-element.17), calls=%async_computation | async-start | bytes 32768 | tf_op jit(solution)/shard_map/all_to_all | solution.py:579
  8.9 1.2 collective-permute-start.1
  9.1 4.7 %collective-permute-start = (f32[168,128]{1,0:T(8,128)}, f32[168,128]{1,0:T(8,128)S(1)}, u32[]{:S(2)}, u32[]{:S(2)}) collective-permute-start(f32[168,128]{1,0:T(8,128)} %get-tuple-element.16), channel_id=1, source_target_pairs={{0,4},{4,0},{1,5},{5,1},{2,6},{6,2},{3,7},{7,3},{8,12},{12,8},{9,1... | collective-permute-start | bytes 258056 | tf_op jit(solution)/shard_map/ppermute | solution.py:533
  10.4 3.4 %copy-start = (f32[168,128]{1,0:T(8,128)S(1)}, f32[168,128]{1,0:T(8,128)}, u32[]{:S(2)}) copy-start(f32[168,128]{1,0:T(8,128)} %get-tuple-element.15.own) | copy-start | bytes 258052
  14.3 24.7 %copy-start.1 = (f32[70,256]{1,0:T(8,128)S(1)}, f32[70,256]{1,0:T(8,128)}, u32[]{:S(2)}) copy-start(f32[70,256]{1,0:T(8,128)} %init_ref) | copy-start | bytes 215044
  14.3 24.7 %copy-start.2 = (f32[40,8]{1,0:T(8,128)S(1)}, f32[40,8]{1,0:T(8,128)}, u32[]{:S(2)}) copy-start(f32[40,8]{1,0:T(8,128)} %get-tuple-element.23.par) | copy-start | bytes 3844
  135.7 3.9 %collective-permute-start.2 = (f32[168,128]{1,0:T(8,128)S(1)}, f32[168,128]{1,0:T(8,128)S(1)}, u32[]{:S(2)}, u32[]{:S(2)}) collective-permute-start(f32[168,128]{1,0:T(8,128)S(1)} %get-tuple-element.25), channel_id=1, source_target_pairs={{0,4},{4,0},{1,5},{5,1},{2,6},{6,2},{3,7},{7,3},{8,12},{12,8},{9,1... | collective-permute-start | bytes 258056 | tf_op jit(solution)/shard_map/ppermute | solution.py:533

commit v8 on v7

--- a/solution.py
+++ b/solution.py
@@ -385,8 +385,8 @@
                 put_fine(ref, e, part)
 
         def substep(n, carry):
-            for u in range(8):
-                substep_one(n * 8 + u)
+            for u in range(16):
+                substep_one(n * 16 + u)
             return carry
 
         def substep_one(n):
@@ -416,7 +416,7 @@
             vel[...] = now
             pos[...] = pos[...] + now
 
-        lax.fori_loop(0, HS * SUB // 8, substep, 0)
+        lax.fori_loop(0, HS * SUB // 16, substep, 0)
         for half, ref in ((0, pos), (PAD, vel)):
             for b, part in enumerate(block_transpose([get_fine(ref, e) for e in range(BLOCKS)])):
                 shift[b, half : half + DOF, :] = part - end[b, half : half + DOF, :]

time: 141 us -> 140 us (level)
  no operation moved by 1% of the time
where the time goes in v8:
time: 140 us
  Pallas kernels  82.3 us (59%)
  blocking collectives  42 us (30%)
  starting transfers between devices  9.91 us (7%)
  waiting for transfers between devices  4.67 us (3%)
    pallas_call x4, Pallas kernels, local_call(): pl.pallas_call(kernel, in_specs=[smem] + [vmem] * len(arrays), out_specs=...  80.5 us
    all_to_all x2, blocking collectives, exchanged(): return lax.all_to_all(value, PEERS, split_axis=0, concat_axis=0, tiled=True)  42 us
    all_to_all x1, starting transfers between devices, shards(): lax.all_to_all(counts, ('c', 'y'), split_axis=0, concat_axis=0, tiled=True)  6.47 us
    ppermute x3, starting transfers between devices, swapped(): return lax.ppermute(value, 'c', [(0, 1), (1, 0)])  3.44 us
    all_to_all x1, waiting for transfers between devices, shards(): lax.all_to_all(counts, ('c', 'y'), split_axis=0, concat_axis=0, tiled=True)  3.12 us
  transfers between devices with their start and end apart: 4, of which 3 were waited for; matrix products, arithmetic and copies ran while one was open for 0% of the time, Pallas kernels for 0%

profile of v8, /device:TPU:1, one launch (start us, length us, event | category | flops | bytes accessed | tf_op | source)
XLA Modules:
  0.0 140.2 jit_solution(10841484896328833289)
XLA Ops:
  0.6 1.7 %split.1 = (f32[8,4,128]{2,1,0:T(4,128)}, f32[40,8]{1,0:T(8,128)}, f32[35,2,35]{2,1,0:T(2,128)}, f32[168,128]{1,0:T(8,128)}, f32[168,128]{1,0:T(8,128)}) custom-call(s32[1]{0:T(128)} %bitcast.core, s32[4,256]{1,0:T(4,128)} %contact.1, f32[35,4,256]{2,1,0:T(4,128)} %bitcast.18, f32[35,2,35]{2,1,0:T(2,128)} %bitcast.19, f32[1,35]{1,0:T(1,128)} %bitcast.20, ...), custom_call_target="tpu_custom_call" | custom-call | tf_op jit(solution)/shard_map/split/pallas_call | solution.py:557
  2.4 0.0 copy-start.3
  2.4 6.5 %all-to-all-start = ((f32[8,4,128]{2,1,0:T(4,128)}), f32[8,4,128]{2,1,0:T(4,128)S(1)}, u32[]{:S(2)}, u32[]{:S(2)}) async-start(f32[8,4,128]{2,1,0:T(4,128)} %get-tuple-element.17), calls=%async_computation | async-start | bytes 32768 | tf_op jit(solution)/shard_map/all_to_all | solution.py:579
  8.9 0.0 copy-done.3
  8.9 0.2 collective-permute-start.1
  9.1 0.3 collective-permute-start
  9.4 0.1 pad_add_fusion.chip
  9.5 0.6 collective-permute-done.1
  10.1 0.1 fusion
  10.2 0.1 rev.3
  10.3 0.1 fusion.1
  10.4 0.0 copy-start
  10.4 0.1 reshape.18
  10.6 0.1 copy.14
  10.6 3.1 %all-to-all-done = f32[8,4,128]{2,1,0:T(4,128)S(1)} async-done(((f32[8,4,128]{2,1,0:T(4,128)}), f32[8,4,128]{2,1,0:T(4,128)S(1)}, u32[]{:S(2)}, u32[]{:S(2)}) %all-to-all-start) | async-done | bytes 16416 | tf_op jit(solution)/shard_map/all_to_all | solution.py:579
  13.8 0.0 collective-permute-done.back
  13.8 0.0 copy-done
  13.8 0.5 pack.1
  14.3 0.0 copy-start.1
  14.3 0.0 copy-start.2
  14.3 24.7 %all_to_all.15.recv = f32[32,32,128]{2,1,0:T(8,128)S(1)} all-to-all(f32[32,32,128]{2,1,0:T(8,128)S(1)} %pack.1), channel_id=1, replica_groups=mesh['x'=4,'z'=8,'c'=2,'y'=4] {'x','z'}, dimensions={0} | all-to-all | bytes 1048576 | tf_op jit(solution)/shard_map/all_to_all | solution.py:537
  39.0 0.0 copy-done.1
  39.0 0.0 copy-done.2
  39.0 79.1 %parareal.1 = f32[32,3,4,128]{3,2,1,0:T(4,128)S(1)} custom-call(s32[2]{0:T(128)S(1)} %pad_add_fusion.chip, f32[70,256]{1,0:T(8,128)S(1)} %copy-done.1, f32[32,32,128]{2,1,0:T(8,128)S(1)} %all_to_all.15.recv, f32[40,8]{1,0:T(8,128)S(1)} %copy-done.2), custom_call_target="tpu_custom_call" | custom-call | tf_op jit(solution)/shard_map/parareal/pallas_call | solution.py:492
  118.1 17.3 %all_to_all.16.recv = f32[32,3,4,128]{3,2,1,0:T(4,128)S(1)} all-to-all(f32[32,3,4,128]{3,2,1,0:T(4,128)S(1)} %parareal.1), channel_id=1, replica_groups=mesh['x'=4,'z'=8,'c'=2,'y'=4] {'x','z'}, dimensions={0} | all-to-all | bytes 393216 | tf_op jit(solution)/shard_map/all_to_all | solution.py:537
  135.4 0.2 unpack.1
  135.6 2.9 %collective-permute-start.2 = (f32[168,128]{1,0:T(8,128)S(1)}, f32[168,128]{1,0:T(8,128)S(1)}, u32[]{:S(2)}, u32[]{:S(2)}) collective-permute-start(f32[168,128]{1,0:T(8,128)S(1)} %get-tuple-element.25), channel_id=1, source_target_pairs={{0,4},{4,0},{1,5},{5,1},{2,6},{6,2},{3,7},{7,3},{8,12},{12,8},{9,1... | collective-permute-start | bytes 258056 | tf_op jit(solution)/shard_map/ppermute | solution.py:533
  138.5 0.9 collective-permute-done.2.back
  139.4 0.7 join.1
  (6 shorter events, 0.0 us)
Async XLA Ops:
  2.4 6.5 %copy-start.3 = (f32[35,2,35]{2,1,0:T(2,128)S(1)}, f32[35,2,35]{2,1,0:T(2,128)}, u32[]{:S(2)}) copy-start(f32[35,2,35]{2,1,0:T(2,128)} %get-tuple-element.18) | copy-start | bytes 29404
  2.4 11.4 %all-to-all-start = ((f32[8,4,128]{2,1,0:T(4,128)}), f32[8,4,128]{2,1,0:T(4,128)S(1)}, u32[]{:S(2)}, u32[]{:S(2)}) async-start(f32[8,4,128]{2,1,0:T(4,128)} %get-tuple-element.17), calls=%async_computation | async-start | bytes 32768 | tf_op jit(solution)/shard_map/all_to_all | solution.py:579
  8.9 1.2 collective-permute-start.1
  9.1 4.7 %collective-permute-start = (f32[168,128]{1,0:T(8,128)}, f32[168,128]{1,0:T(8,128)S(1)}, u32[]{:S(2)}, u32[]{:S(2)}) collective-permute-start(f32[168,128]{1,0:T(8,128)} %get-tuple-element.16), channel_id=1, source_target_pairs={{0,4},{4,0},{1,5},{5,1},{2,6},{6,2},{3,7},{7,3},{8,12},{12,8},{9,1... | collective-permute-start | bytes 258056 | tf_op jit(solution)/shard_map/ppermute | solution.py:533
  10.4 3.4 %copy-start = (f32[168,128]{1,0:T(8,128)S(1)}, f32[168,128]{1,0:T(8,128)}, u32[]{:S(2)}) copy-start(f32[168,128]{1,0:T(8,128)} %get-tuple-element.15.own) | copy-start | bytes 258052
  14.3 24.7 %copy-start.1 = (f32[70,256]{1,0:T(8,128)S(1)}, f32[70,256]{1,0:T(8,128)}, u32[]{:S(2)}) copy-start(f32[70,256]{1,0:T(8,128)} %init_ref) | copy-start | bytes 215044
  14.3 24.7 %copy-start.2 = (f32[40,8]{1,0:T(8,128)S(1)}, f32[40,8]{1,0:T(8,128)}, u32[]{:S(2)}) copy-start(f32[40,8]{1,0:T(8,128)} %get-tuple-element.23.par) | copy-start | bytes 3844
  135.6 3.9 %collective-permute-start.2 = (f32[168,128]{1,0:T(8,128)S(1)}, f32[168,128]{1,0:T(8,128)S(1)}, u32[]{:S(2)}, u32[]{:S(2)}) collective-permute-start(f32[168,128]{1,0:T(8,128)S(1)} %get-tuple-element.25), channel_id=1, source_target_pairs={{0,4},{4,0},{1,5},{5,1},{2,6},{6,2},{3,7},{7,3},{8,12},{12,8},{9,1... | collective-permute-start | bytes 258056 | tf_op jit(solution)/shard_map/ppermute | solution.py:533
